TPU v7x, 128 devices: a whole 4x4x4 slice. The times are simulated.
128 devices in a mesh: row: 8 (over y, core), col: 16 (over x, z).
Axes of the slice: x: 4, y: 4, z: 4, core: 2. Of those that a mesh axis runs over, the one named last changes fastest.
Arguments:
- coupling_panel: bfloat16 [8, 1536, 512], P('row'), may hold values from -6 to 6
- interior_factor: float32 [8, 1536, 1536], P('row'), may hold values from -1 to 3, as said below
- border_rows: bfloat16 [8, 8192, 1536], P('row', 'col'), may hold values from -0.109375 to 0.109375
- target_rows: int32 [8, 8192], P('row', 'col'), may hold values from 0 to 32767, as said below
- border_block: float32 [32768, 512], P(('row', 'col')), may hold values from -6 to 6
Outputs:
- schur_panel: float32 [32768, 512], P(('row', 'col'))
Inputs may be any that keep to these rules, and one draw needn't show every extreme that they name: `target_rows`: each block of 512 entries along the second dimension (the rows of one device) is nondecreasing. Row g of the Schur panel is held by device g // 256 in the order of row+col. The rows of one device name any one holder at most 8 times, and some holder is named exactly 8 times by the rows of every device. `interior_factor`: each [1536, 1536] block is lower triangular with diagonal entries between 1 and 3.
All inputs are finite; a program needn't handle non-finite values.
Results may differ from a plain program's by a relative error of at most 0.0029.
Values may be sent and summed in bfloat16 or wider, within the bound.
A program may use at most 128 MiB of HBM per device.

v0:
```python
import jax
import jax.numpy as jnp
from jax import lax
from jax.sharding import PartitionSpec as P


def substitute(factor, panel_cols):
    forward = lax.linalg.triangular_solve(factor, panel_cols, left_side=True, lower=True)
    return lax.linalg.triangular_solve(
        factor, forward, left_side=True, lower=True, transpose_a=True
    )


def local(coupling_panel, interior_factor, border_rows, target_rows, border_block):
    factor = interior_factor[0]
    panel_cols = coupling_panel[0]
    coupling_rows = border_rows[0]
    targets = target_rows[0]
    panel_width = panel_cols.shape[1]
    holders = lax.axis_size("row") * lax.axis_size("col")
    owned_rows = border_block.shape[0]
    sent_rows = targets.shape[0]
    slot_depth = 2 * sent_rows // holders
    holder_of = targets // owned_rows
    onehot = (holder_of[:, None] == jnp.arange(holders, dtype=jnp.int32)[None, :]).astype(jnp.int32)
    counts = jnp.sum(onehot, axis=0)
    starts = jnp.cumsum(counts) - counts
    start_of = jnp.sum(onehot * starts[None, :], axis=1)
    slot_rank = jnp.arange(sent_rows, dtype=jnp.int32) - start_of
    position = holder_of * slot_depth + slot_rank
    within = targets - holder_of * owned_rows
    send_index = jnp.zeros((holders * slot_depth,), jnp.int32).at[position].set(within)
    recv_index = lax.all_to_all(
        send_index.reshape(holders, slot_depth),
        ("row", "col"),
        split_axis=0,
        concat_axis=0,
        tiled=True,
    )
    solved = substitute(factor, panel_cols.astype(jnp.float32)).astype(jnp.bfloat16)
    update = jnp.dot(coupling_rows, solved, preferred_element_type=jnp.float32)
    outgoing = jnp.zeros((holders * slot_depth, panel_width), jnp.float32).at[position].set(update)
    received = lax.all_to_all(
        outgoing.reshape(holders, slot_depth, panel_width),
        ("row", "col"),
        split_axis=0,
        concat_axis=0,
        tiled=True,
    )
    received = received.reshape(holders * slot_depth, panel_width)
    assembled = (
        jnp.zeros((owned_rows, panel_width), jnp.float32).at[recv_index.reshape(-1)].add(received)
    )
    return border_block - assembled


def solution(mesh):
    placed = (
        P("row", None, None),
        P("row", None, None),
        P("row", "col", None),
        P("row", "col"),
        P(("row", "col"), None),
    )
    return jax.shard_map(
        local, mesh=mesh, in_specs=placed, out_specs=P(("row", "col"), None), check_vma=False
    )
```

profile of v0, /device:TPU:1, one launch (start us, length us, event | category | flops | bytes accessed | tf_op | source)
XLA Modules:
  0.0 275.9 jit_solution(8107232784915928413)
XLA Ops:
  0.0 0.8 multiply_subtract_fusion
  1.6 0.7 compare_select_fusion.1
  2.3 2.4 scatter_custom_fusion
  4.8 0.7 all_to_all.9
  5.5 11.5 %all-to-all-start = ((s32[128,1,8]{2,1,0:T(1,128)}), s32[128,1,8]{2,1,0:T(1,128)S(1)}, u32[]{:S(2)}, u32[]{:S(2)}) async-start(s32[128,1,8]{2,1,0:T(1,128)} %bitcast.5), calls=%async_computation | async-start | bytes 131072 | tf_op jit(solution)/shard_map/all_to_all | solution.py:33
  17.0 8.4 %bitcast_select_fusion = f32[1536,1536]{1,0:T(8,128)} fusion(f32[1,1536,1536]{2,1,0:T(8,128)} %param.6), kind=kLoop, calls=%fused_computation.5 | loop fusion | flops 4718592 | bytes 18874368 | tf_op jit(solution)/shard_map/triangular_solve | solution.py:9
  25.4 36.0 %while.1 = (s32[]{:T(128)}, f32[1536,1536]{1,0:T(8,128)}, s32[12,2]{0,1:T(2,128)S(1)}, f32[12,128,128]{2,1,0:T(8,128)S(1)}, s32[]{:T(128)}) while((s32[]{:T(128)}, f32[1536,1536]{1,0:T(8,128)}, s32[12,2]{0,1:T(2,128)S(1)}, f32[12,128,128]{2,1,0:T(8,128)S(1)}, s32[]{:T(128)}) %tuple.84), condition=%wide.while_cond, body=%wide.while_body.sunk | while | flops 2 | bytes 131181 | solution.py:9
  25.4 0.6 fusion.140
  26.0 2.3 bitcast_dynamic-update-slice_fusion.2
  28.4 0.6 fusion.140
  29.0 2.3 bitcast_dynamic-update-slice_fusion.2
  31.4 0.6 fusion.140
  32.0 2.3 bitcast_dynamic-update-slice_fusion.2
  34.5 0.6 fusion.140
  35.0 2.3 bitcast_dynamic-update-slice_fusion.2
  37.5 0.6 fusion.140
  38.1 2.3 bitcast_dynamic-update-slice_fusion.2
  40.5 0.6 fusion.140
  41.1 2.3 bitcast_dynamic-update-slice_fusion.2
  43.5 0.6 fusion.140
  44.1 2.3 bitcast_dynamic-update-slice_fusion.2
  46.5 0.6 fusion.140
  47.1 2.3 bitcast_dynamic-update-slice_fusion.2
  49.5 0.6 fusion.140
  50.1 2.3 bitcast_dynamic-update-slice_fusion.2
  52.5 0.6 fusion.140
  53.1 2.3 bitcast_dynamic-update-slice_fusion.2
  55.5 0.6 fusion.140
  56.1 2.3 bitcast_dynamic-update-slice_fusion.2
  58.5 0.6 fusion.140
  59.1 2.2 bitcast_dynamic-update-slice_fusion.2
  61.3 118.0 %custom-call.5 = f32[12,128,128]{1,2,0:T(8,128)S(1)} custom-call(f32[12,128,128]{2,1,0:T(8,128)S(1)} %get-tuple-element.12), custom_call_target="InvertDiagBlocksLowerTriangular" | custom-call | tf_op jit(solution)/shard_map/triangular_solve | solution.py:9
  179.4 2.0 convert_element_type.9
  181.4 1.7 constant_dynamic-update-slice_fusion.44
  183.1 1.2 convolution_subtract_fusion.11
  184.4 0.5 constant_dynamic-update-slice_fusion.43
  185.3 0.5 constant_dynamic-update-slice_fusion.42
  185.9 0.6 convolution_subtract_fusion.17
  187.1 0.7 convolution_subtract_fusion.21
  187.8 0.5 constant_dynamic-update-slice_fusion.40
  188.3 0.9 convolution_subtract_fusion.9
  189.8 1.0 convolution_subtract_fusion.16
  191.3 1.2 convolution_subtract_fusion.8
  193.0 1.3 convolution_subtract_fusion.7
  194.7 1.5 convolution_subtract_fusion.15
  196.7 1.8 convolution_subtract_fusion.20
  198.9 1.8 convolution_subtract_fusion.6
  203.1 0.7 convolution_subtract_fusion.14
  204.2 0.8 convolution_subtract_fusion.19
  205.5 1.0 convolution_subtract_fusion.3
  207.0 1.1 convolution_subtract_fusion.13
  208.7 1.3 convolution_subtract_fusion.2
  210.6 1.9 convolution_subtract_fusion.1
  213.1 1.6 convolution_subtract_fusion.12
  215.3 1.8 convolution_subtract_fusion.18
  217.8 2.0 convolution_subtract_fusion
  220.4 2.0 fusion.4
  222.4 1.6 copy.15
  224.0 3.6 %scatter_custom_fusion.1 = f32[1024,512]{1,0:T(8,128)} fusion(s32[512]{0:T(512)S(1)} %bitcast.218, f32[512,512]{1,0:T(8,128)S(1)} %copy.15, f32[]{:T(128)} %constant.36.clone.1), kind=kCustom, calls=%fused_computation.50 | custom fusion | bytes 2097156 | tf_op jit(solution)/shard_map/scatter | solution.py:42
  227.6 10.6 %all-to-all-start.1 = ((f32[128,8,512]{2,1,0:T(8,128)}), f32[128,8,512]{2,1,0:T(8,128)}, u32[]{:S(2)}, u32[]{:S(2)}) async-start(f32[128,8,512]{2,1,0:T(8,128)} %bitcast.212), calls=%async_computation.1 | async-start | bytes 4194304 | tf_op jit(solution)/shard_map/all_to_all | solution.py:43
  238.7 0.8 reduce.4
  239.7 27.6 %all-to-all-done.1 = f32[128,8,512]{2,1,0:T(8,128)} async-done(((f32[128,8,512]{2,1,0:T(8,128)}), f32[128,8,512]{2,1,0:T(8,128)}, u32[]{:S(2)}, u32[]{:S(2)}) %all-to-all-start.1) | async-done | bytes 2097184 | tf_op jit(solution)/shard_map/all_to_all | solution.py:43
  267.3 7.5 %scatter_custom_fusion.2 = f32[256,512]{1,0:T(8,128)S(1)} fusion(s32[1024]{0:T(1024)S(1)} %bitcast.215, f32[128,8,512]{2,1,0:T(8,128)} %all-to-all-done.1, f32[]{:T(128)} %constant.36.clone.1), kind=kCustom, calls=%fused_computation.7 | custom fusion | flops 524288 | bytes 2621444 | tf_op jit(solution)/shard_map/scatter-add | solution.py:52
  274.8 0.9 sub.36
  (114 shorter events, 13.0 us)
Async XLA Ops:
  0.0 220.4 %copy-start = (bf16[1,512,1536]{2,1,0:T(8,128)(2,1)S(1)}, bf16[1,512,1536]{2,1,0:T(8,128)(2,1)}, u32[]{:S(2)}) copy-start(bf16[1,512,1536]{2,1,0:T(8,128)(2,1)} %param.7) | copy-start | bytes 4718596
  5.5 222.1 %all-to-all-start = ((s32[128,1,8]{2,1,0:T(1,128)}), s32[128,1,8]{2,1,0:T(1,128)S(1)}, u32[]{:S(2)}, u32[]{:S(2)}) async-start(s32[128,1,8]{2,1,0:T(1,128)} %bitcast.5), calls=%async_computation | async-start | bytes 131072 | tf_op jit(solution)/shard_map/all_to_all | solution.py:33
  179.4 5.5 %copy-start.1 = (f32[1536,1536]{1,0:T(8,128)S(1)}, f32[1536,1536]{1,0:T(8,128)}, u32[]{:S(2)}) copy-start(f32[1536,1536]{1,0:T(8,128)} %get-tuple-element.152) | copy-start | bytes 28311556
  227.6 39.7 %all-to-all-start.1 = ((f32[128,8,512]{2,1,0:T(8,128)}), f32[128,8,512]{2,1,0:T(8,128)}, u32[]{:S(2)}, u32[]{:S(2)}) async-start(f32[128,8,512]{2,1,0:T(8,128)} %bitcast.212), calls=%async_computation.1 | async-start | bytes 4194304 | tf_op jit(solution)/shard_map/all_to_all | solution.py:43
  238.2 36.6 %copy-start.2 = (f32[256,512]{1,0:T(8,128)S(1)}, f32[256,512]{1,0:T(8,128)}, u32[]{:S(2)}) copy-start(f32[256,512]{1,0:T(8,128)} %param.9) | copy-start | bytes 1572868
where the time goes:
time: 281 us; the launch traced here: 276 us
  other arithmetic  140 us (50%)
  local copies, waits for them, and re-layouts  45.8 us (16%)
  matrix products  39 us (14%)
  waiting for transfers between devices  27.6 us (10%)
  starting transfers between devices  22.1 us (8%)
    another operation x4, other arithmetic, substitute(): lax.linalg.triangular_solve(factor, forward, left_side=True, lower=True,...  126 us
    another operation x37, local copies, waits for them, and re-layouts  35.9 us
    all_to_all x1, waiting for transfers between devices, local(): lax.all_to_all(outgoing.reshape(holders, slot_depth, panel_width), ('row'...  27.6 us
    another operation x23, matrix products, substitute(): lax.linalg.triangular_solve(factor, panel_cols, left_side=True, lower=True)  19.5 us
    another operation x23, matrix products, substitute(): lax.linalg.triangular_solve(factor, forward, left_side=True, lower=True,...  17.4 us
    all_to_all x1, starting transfers between devices, local(): lax.all_to_all(send_index.reshape(holders, slot_depth), ('row', 'col'), s...  11.5 us
    all_to_all x1, starting transfers between devices, local(): lax.all_to_all(outgoing.reshape(holders, slot_depth, panel_width), ('row'...  10.6 us
    scatter-add x1, other arithmetic, local(): jnp.zeros((owned_rows, panel_width), jnp.float32).at[recv_index.reshape(-1)]  7.51 us
  transfers between devices with their start and end apart: 2, of which 1 were waited for; matrix products, arithmetic and copies ran while one was open for 76% of the time, Pallas kernels for 0%

commit v1 on v0

v1 whole, which is shorter than its diff:
```python
import jax
import jax.numpy as jnp
from jax import lax
from jax.experimental import pallas as pl
from jax.experimental.pallas import tpu as pltpu
from jax.sharding import PartitionSpec as P

F32, BF16, I32 = jnp.float32, jnp.bfloat16, jnp.int32
BASE = 32
TILE = 256
BIG = 512
CHUNK = 256
SLOTS = 8
LOGICAL = pl.DeviceIdType.LOGICAL
EMPTY = -512.0


def iota(shape, axis):
    return lax.broadcasted_iota(I32, shape, axis)


def split(x):
    hi = x.astype(BF16)
    return hi, (x - hi.astype(F32)).astype(BF16)


def mm(a, b):
    return jnp.dot(a, b, preferred_element_type=F32)


def mm_nt(a, b):
    return lax.dot_general(a, b, (((1,), (1,)), ((), ())), preferred_element_type=F32)


def mm3(a, b):
    return mm(a[0], b[0]) + (mm(a[0], b[1]) + mm(a[1], b[0]))


def invert_base(strip):
    rows, width = strip.shape
    lane = iota((rows, width), 1)
    row = iota((rows, width), 0)
    within = lane % BASE
    start = lane - within
    tiles = range(0, width, 128)
    local = (lane - within)[:, :128] % 128

    def pick(x, index):
        return jnp.concatenate(
            [jnp.take_along_axis(x[:, t : t + 128], index[: x.shape[0]], axis=1) for t in tiles], axis=1
        )

    recip = 1.0 / pick(strip, local + row[:, :128])
    scaled = jnp.where(within < row, strip * recip, 0.0)
    inverse = jnp.where(within == row, recip, 0.0)
    for k in range(rows - 1):
        first = (k + 1) // 8 * 8
        factor = pick(scaled[first:], local + k)
        update = inverse[first:] - factor * inverse[k : k + 1]
        inverse = update if first == 0 else jnp.concatenate([inverse[:first], update], axis=0)
    return inverse


def merge_mask(size):
    r, c = iota((TILE, TILE), 0), iota((TILE, TILE), 1)
    return (r // (2 * size) == c // (2 * size)) & (r // size % 2 == 1) & (c // size % 2 == 0)


def kernel(
    panel_ref, factor_ref, rows_ref, target_ref, block_ref, out_ref,
    diag, sub, off, vh, vl, oh, ol, fwd, sol, place, send, recv, send_idx, recv_idx,
    load_sem, send_sem, recv_sem,
):
    n_holders = lax.axis_size("row") * lax.axis_size("col")
    me = lax.axis_index("row") * lax.axis_size("col") + lax.axis_index("col")
    n_big = off.shape[0]
    n_tile = diag.shape[0]
    pairs = [(1, 0), (2, 0), (2, 1)]

    loads = []

    def load(src_rows, src_cols, dst, sem):
        cp = pltpu.make_async_copy(factor_ref.at[src_rows, src_cols], dst, sem)
        cp.start()
        return cp

    load_diag = [
        load(pl.ds(t * TILE, TILE), pl.ds(t * TILE, TILE), diag.at[t], load_sem.at[t]) for t in range(n_tile)
    ]
    load_sub = [
        load(pl.ds((2 * t + 1) * TILE, TILE), pl.ds(2 * t * TILE, TILE), sub.at[t], load_sem.at[n_tile + t])
        for t in range(n_big)
    ]
    load_off = [
        load(pl.ds(i * BIG, BIG), pl.ds(j * BIG, BIG), off.at[p], load_sem.at[n_tile + n_big + p])
        for p, (i, j) in enumerate(pairs)
    ]

    barrier = pltpu.get_barrier_semaphore()

    def greet(o, carry):
        pl.semaphore_signal(barrier, inc=1, device_id=lax.rem(me + o, n_holders), device_id_type=LOGICAL)
        return carry

    lax.fori_loop(1, n_holders, greet, 0)

    sent = target_ref.shape[1]
    target = jnp.broadcast_to(target_ref[...], (8, sent))
    holder = target // block_ref.shape[0]
    within = target - holder * block_ref.shape[0]
    lane = iota((8, sent), 1)
    rank = jnp.zeros((8, sent), I32)
    for d in range(1, SLOTS):
        same = (pltpu.roll(holder, d, 1) == holder) & (lane >= d)
        rank = rank + jnp.where(same, 1, 0)
    position = (holder * SLOTS + rank)[:1]
    slots = n_holders * SLOTS
    placed = jnp.where(iota((slots, sent), 0) == position, 1.0, 0.0).astype(BF16)
    place[...] = placed
    described = jnp.concatenate(
        [jnp.broadcast_to(within[:1].astype(F32), (128, sent)), jnp.ones((128, sent), F32)], axis=0
    ).astype(BF16)
    found = mm_nt(placed, described)
    index = (found[:, :128] + EMPTY * (1.0 - found[:, 128:])).reshape(n_holders, SLOTS, 128)
    send_idx[...] = jnp.concatenate([index, index], axis=1).astype(BF16)

    for cp in load_diag:
        cp.wait()
    parts = []
    group = iota((BASE, 128), 1) // BASE
    for t in range(n_tile):
        for half in range(2):
            lo = half * 128
            tile = diag[t, lo : lo + 128, lo : lo + 128]
            strip = tile[:BASE]
            for q in range(1, 128 // BASE):
                strip = jnp.where(group == q, tile[q * BASE : (q + 1) * BASE], strip)
            parts.append(strip)
    base = invert_base(jnp.concatenate(parts, axis=1))
    wide = iota((BASE, TILE), 1) // BASE
    inverse = []
    for t in range(n_tile):
        piece = base[:, t * TILE : (t + 1) * TILE]
        inverse.append(
            jnp.concatenate([jnp.where(wide == q, piece, 0.0) for q in range(TILE // BASE)], axis=0)
        )
    size = BASE
    while size < TILE:
        mask = merge_mask(size)
        for t in range(n_tile):
            v = split(inverse[t])
            low = split(jnp.where(mask, diag[t], 0.0))
            inverse[t] = inverse[t] - mm3(v, split(mm3(low, v)))
        size *= 2
    for cp in load_sub:
        cp.wait()
    for b in range(n_big):
        top, bottom = split(inverse[2 * b]), split(inverse[2 * b + 1])
        left = split(mm3(bottom, split(mm3(split(sub[b]), top))))
        for ref, i, sign in ((vh, 0, 1), (vl, 1, 1)):
            ref[b, :TILE, :TILE] = top[i]
            ref[b, TILE:, TILE:] = bottom[i]
            ref[b, TILE:, :TILE] = -left[i]

    for p in range(len(pairs)):
        load_off[p].wait()
        oh[p], ol[p] = split(off[p])

    pl.semaphore_wait(barrier, n_holders - 1)

    def dispatch(source, target_buf, sem_at):
        def one(o, carry):
            to = lax.rem(me + o, n_holders)
            pltpu.make_async_remote_copy(
                src_ref=source.at[to],
                dst_ref=target_buf.at[me],
                send_sem=send_sem.at[sem_at],
                recv_sem=recv_sem.at[sem_at],
                device_id=to,
                device_id_type=LOGICAL,
            ).start()
            return carry

        lax.fori_loop(1, n_holders, one, 0)
        target_buf[me] = source[me]

    def arrived(source, target_buf, sem_at):
        others = pl.ds(0, n_holders - 1)
        pltpu.make_async_copy(source.at[others], target_buf.at[others], recv_sem.at[sem_at]).wait()

    def left_device(source, target_buf, sem_at):
        others = pl.ds(0, n_holders - 1)
        pltpu.make_async_copy(source.at[others], target_buf.at[others], send_sem.at[sem_at]).wait()

    dispatch(send_idx, recv_idx, 0)

    def block_inv(b):
        return (vh[b], vl[b])

    n_chunk = send.shape[0]
    for ch in range(n_chunk):
        cols = slice(ch * CHUNK, (ch + 1) * CHUNK)
        rhs = [panel_ref[b * BIG : (b + 1) * BIG, cols].astype(F32) for b in range(n_big)]
        for b in range(n_big):
            r = split(rhs[b])
            v = block_inv(b)
            upper = mm3((v[0][:TILE, :TILE], v[1][:TILE, :TILE]), (r[0][:TILE], r[1][:TILE]))
            lower = mm3((v[0][TILE:], v[1][TILE:]), r)
            f = jnp.concatenate([upper, lower], axis=0)
            fwd[:, b * BIG : (b + 1) * BIG] = f.T
            fs = split(f)
            for p, (i, j) in enumerate(pairs):
                if j == b:
                    rhs[i] = rhs[i] - mm3((oh[p], ol[p]), fs)
        for b in reversed(range(n_big)):
            q = split(fwd[:, b * BIG : (b + 1) * BIG])
            v = block_inv(b)
            first = mm3(q, (v[0][:, :TILE], v[1][:, :TILE]))
            second = mm3((q[0][:, TILE:], q[1][:, TILE:]), (v[0][TILE:, TILE:], v[1][TILE:, TILE:]))
            x = jnp.concatenate([first, second], axis=1)
            xs = split(x)
            sol[:, b * BIG : (b + 1) * BIG] = xs[0]
            for p, (i, j) in enumerate(pairs):
                if i == b:
                    at = slice(j * BIG, (j + 1) * BIG)
                    fwd[:, at] = fwd[:, at] - mm3(xs, (oh[p], ol[p]))
        update = mm_nt(rows_ref[...], sol[...]).astype(BF16)
        packed = mm(place[...], update).reshape(n_holders, SLOTS, CHUNK)
        send[ch] = jnp.concatenate([packed[:, :, :128], packed[:, :, 128:]], axis=1).astype(BF16)
        dispatch(send.at[ch], recv.at[ch], 1 + ch)

    arrived(send_idx, recv_idx, 0)
    owned = block_ref.shape[0]
    pick0 = jnp.where(iota((8, 128), 1) == 0, 1.0, 0.0).astype(BF16)
    named = mm_nt(pick0, recv_idx[...].reshape(n_holders * 2 * SLOTS, 128))[:1]
    total = n_holders * 2 * SLOTS
    named = named + jnp.where(iota((1, total), 1) // SLOTS % 2 == 1, float(owned), 0.0)
    gather = jnp.where(iota((2 * owned, total), 0).astype(F32) == named, 1.0, 0.0).astype(BF16)
    for ch in range(n_chunk):
        arrived(send.at[ch], recv.at[ch], 1 + ch)
        summed = mm(gather, recv[ch].reshape(total, 128))
        for half in range(2):
            cols = slice(ch * CHUNK + half * 128, ch * CHUNK + (half + 1) * 128)
            out_ref[:, cols] = block_ref[:, cols] - summed[half * owned : (half + 1) * owned]
    left_device(send_idx, recv_idx, 0)
    for ch in range(n_chunk):
        left_device(send.at[ch], recv.at[ch], 1 + ch)


def local(coupling_panel, interior_factor, border_rows, target_rows, border_block):
    panel, factor, rows = coupling_panel[0], interior_factor[0], border_rows[0]
    n, width = panel.shape
    holders = lax.axis_size("row") * lax.axis_size("col")
    n_tile, n_big, n_chunk = n // TILE, n // BIG, width // CHUNK
    pairs = n_big * (n_big - 1) // 2
    vmem = pl.BlockSpec(memory_space=pltpu.VMEM)
    return pl.pallas_call(
        kernel,
        out_shape=jax.ShapeDtypeStruct(border_block.shape, F32),
        in_specs=[vmem, pl.BlockSpec(memory_space=pl.ANY), vmem, vmem, vmem],
        out_specs=vmem,
        scratch_shapes=[
            pltpu.VMEM((n_tile, TILE, TILE), F32),
            pltpu.VMEM((n_big, TILE, TILE), F32),
            pltpu.VMEM((pairs, BIG, BIG), F32),
            pltpu.VMEM((n_big, BIG, BIG), BF16),
            pltpu.VMEM((n_big, BIG, BIG), BF16),
            pltpu.VMEM((pairs, BIG, BIG), BF16),
            pltpu.VMEM((pairs, BIG, BIG), BF16),
            pltpu.VMEM((CHUNK, n), F32),
            pltpu.VMEM((CHUNK, n), BF16),
            pltpu.VMEM((holders * SLOTS, target_rows.shape[1]), BF16),
            pltpu.VMEM((n_chunk, holders, 2 * SLOTS, 128), BF16),
            pltpu.VMEM((n_chunk, holders, 2 * SLOTS, 128), BF16),
            pltpu.VMEM((holders, 2 * SLOTS, 128), BF16),
            pltpu.VMEM((holders, 2 * SLOTS, 128), BF16),
            pltpu.SemaphoreType.DMA((n_tile + n_big + pairs,)),
            pltpu.SemaphoreType.DMA((1 + n_chunk,)),
            pltpu.SemaphoreType.DMA((1 + n_chunk,)),
        ],
        compiler_params=pltpu.CompilerParams(
            collective_id=0, has_side_effects=True, vmem_limit_bytes=60 * 1024 * 1024
        ),
        name="schur_panel",
    )(panel, factor, rows, target_rows, border_block)


def solution(mesh):
    placed = (
        P("row", None, None),
        P("row", None, None),
        P("row", "col", None),
        P("row", "col"),
        P(("row", "col"), None),
    )
    return jax.shard_map(
        local, mesh=mesh, in_specs=placed, out_specs=P(("row", "col"), None), check_vma=False
    )
```

time: 281 us -> 50.5 us (0.18); the launches traced: 276 us -> 50.3 us
  other arithmetic: 140 us -> 0 us
  Pallas kernels: 0 us -> 48.5 us
  local copies, waits for them, and re-layouts: 45.8 us -> 1.87 us
  matrix products: 39 us -> 0 us
  waiting for transfers between devices: 27.6 us -> 0 us
  starting transfers between devices: 22.1 us -> 0 us
    another operation x6 -> x0, other arithmetic: 127 us -> none  [the longest x4 126 us: substitute(): lax.linalg.triangular_solve(factor, forward, left_side=True, lower=True,...]
    pallas_call x0 -> x1, Pallas kernels: none -> 48.5 us  [local(): pl.pallas_call(kernel, out_shape=jax.ShapeDtypeStruct(border_block.shape,...]
    another operation x46 -> x0, matrix products: 37 us -> none  [the longest x23 19.5 us: substitute(): lax.linalg.triangular_solve(factor, panel_cols, left_side=True, lower=True)]
    another operation x45 -> x0, local copies, waits for them, and re-layouts: 36 us -> none
    all_to_all x2 -> x0, waiting for transfers between devices: 27.6 us -> none  [the longest x1 27.6 us: local(): lax.all_to_all(outgoing.reshape(holders, slot_depth, panel_width), ('row'...]
    all_to_all x2 -> x0, starting transfers between devices: 22.1 us -> none  [the longest x1 11.5 us: local(): lax.all_to_all(send_index.reshape(holders, slot_depth), ('row', 'col'), s...]
    scatter-add x1 -> x0, other arithmetic: 7.51 us -> none  [local(): jnp.zeros((owned_rows, panel_width), jnp.float32).at[recv_index.reshape(-1)]]
    scatter x2 -> x0, local copies, waits for them, and re-layouts: 6.09 us -> none  [the longest x1 3.64 us: local(): jnp.zeros((holders * slot_depth, panel_width), jnp.float32).at[position]]
  transfers between devices with their start and end apart: 2 -> 0, of which waited for: 1 -> 0; matrix products, arithmetic and copies ran while one was open for 76% -> 0% of each run, Pallas kernels for 0% -> 0%
where the time goes in v1:
time: 50.5 us; the launch traced here: 50.3 us
  Pallas kernels  48.5 us (96%)
  local copies, waits for them, and re-layouts  1.87 us (4%)
    pallas_call x1, Pallas kernels, local(): pl.pallas_call(kernel, out_shape=jax.ShapeDtypeStruct(border_block.shape,...  48.5 us
    unnamed x1, local copies, waits for them, and re-layouts  1.87 us

profile of v1, /device:TPU:1, one launch (start us, length us, event | category | flops | bytes accessed | tf_op | source)
XLA Modules:
  0.0 50.3 jit_solution(13796503766866170593)
XLA Ops:
  0.0 48.5 %schur_panel.1 = f32[256,512]{1,0:T(8,128)} custom-call(bf16[1536,512]{1,0:T(8,128)(2,1)} %bitcast.4, f32[1536,1536]{1,0:T(8,128)} %bitcast.3, bf16[512,1536]{1,0:T(8,128)(2,1)} %bitcast.5, s32[1,512]{1,0:T(1,128)} %target_ref.1, f32[256,512]{1,0:T(8,128)} %block_ref.1), custom_call_target="tpu_custom_call" | custom-call | tf_op jit(solution)/shard_map/schur_panel/pallas_call | solution.py:257
  48.5 1.9 %copy.7 = f32[256,512]{1,0:T(8,128)} copy(f32[256,512]{1,0:T(8,128)} %schur_panel.1) | data formatting | bytes 1048576

commit v2 on v1

v2 whole, which is shorter than its diff:
```python
import jax
import jax.numpy as jnp
from jax import lax
from jax.experimental import pallas as pl
from jax.experimental.pallas import tpu as pltpu
from jax.sharding import PartitionSpec as P

F32, BF16, I32 = jnp.float32, jnp.bfloat16, jnp.int32
BASE = 32
TILE = 256
BIG = 512
CHUNK = 256
SLOTS = 8
GROUPS = 4
LOGICAL = pl.DeviceIdType.LOGICAL
EMPTY = -512.0


def iota(shape, axis):
    return lax.broadcasted_iota(I32, shape, axis)


def split(x):
    hi = x.astype(BF16)
    return hi, (x - hi.astype(F32)).astype(BF16)


def mm(a, b):
    return jnp.dot(a, b, preferred_element_type=F32)


def mm_nt(a, b):
    return lax.dot_general(a, b, (((1,), (1,)), ((), ())), preferred_element_type=F32)


def mm3(a, b):
    return mm(a[0], b[0]) + (mm(a[0], b[1]) + mm(a[1], b[0]))


def invert_base(strip):
    rows, width = strip.shape
    lane = iota((rows, width), 1)
    row = iota((rows, width), 0)
    within = lane % BASE
    start = lane - within
    tiles = range(0, width, 128)
    local = (lane - within)[:, :128] % 128

    def pick(x, index):
        return jnp.concatenate(
            [jnp.take_along_axis(x[:, t : t + 128], index[: x.shape[0]], axis=1) for t in tiles], axis=1
        )

    recip = 1.0 / pick(strip, local + row[:, :128])
    scaled = jnp.where(within < row, strip * recip, 0.0)
    inverse = jnp.where(within == row, recip, 0.0)
    for k in range(rows - 1):
        first = (k + 1) // 8 * 8
        factor = pick(scaled[first:], local + k)
        update = inverse[first:] - factor * inverse[k : k + 1]
        inverse = update if first == 0 else jnp.concatenate([inverse[:first], update], axis=0)
    return inverse


def spread(strip, size):
    if size == TILE:
        return strip
    group = iota((size, TILE), 1) // size
    return tuple(
        jnp.concatenate(
            [part * jnp.where(group == q, 1.0, 0.0).astype(BF16) for q in range(TILE // size)], axis=0
        )
        for part in strip
    )


def below(corner, first, second, size):
    inner = mm3(split(corner), spread(split(first), size))
    return -mm3(split(second), spread(split(inner), size))


def widen(tiles):
    return [jnp.concatenate(tiles[t : t + 2], axis=1) for t in range(0, len(tiles), 2)]


def narrow(strips):
    return [w[:, h : h + 128] for w in strips for h in (0, 128)]


def invert(diag):
    n_tile = diag.shape[0]
    small = [
        diag[t, h : h + 128, h : h + 128] for t in range(n_tile) for h in range(0, TILE, 128)
    ]
    group = iota((BASE, 128), 1) // BASE
    strips = []
    for tile in small:
        strip = tile[:BASE]
        for q in range(1, 128 // BASE):
            strip = jnp.where(group == q, tile[q * BASE : (q + 1) * BASE], strip)
        strips.append(strip)
    base = invert_base(jnp.concatenate(strips, axis=1))
    tiles = [base[:, t : t + 128] for t in range(0, base.shape[1], 128)]
    size = BASE
    while size < 128:
        group = iota((size, 128), 1) // size
        even = group % 2 == 0
        corners = []
        for tile in small:
            corner = tile[size : 2 * size]
            for q in range(1, 128 // (2 * size)):
                at = (2 * q + 1) * size
                corner = jnp.where(group == 2 * q, tile[at : at + size], corner)
            corners.append(corner)

        def evens(x):
            return [jnp.where(even, x[t], pltpu.roll(x[t + 1], size, 1)) for t in range(0, len(x), 2)]

        def odds(x):
            return [jnp.where(even, pltpu.roll(x[t], 128 - size, 1), x[t + 1]) for t in range(0, len(x), 2)]

        left = narrow(
            [
                below(c, f, g, size)
                for c, f, g in zip(widen(evens(corners)), widen(evens(tiles)), widen(odds(tiles)))
            ]
        )
        merged = []
        for t, tile in enumerate(tiles):
            x = left[t // 2] if t % 2 == 0 else pltpu.roll(left[t // 2], 128 - size, 1)
            merged.append(
                jnp.concatenate([jnp.where(even, tile, 0.0), jnp.where(even, x, tile)], axis=0)
            )
        tiles = merged
        size *= 2
    corners = [diag[t, 128:, :128] for t in range(n_tile)]
    left = narrow(
        [below(c, f, g, 128) for c, f, g in zip(widen(corners), widen(tiles[::2]), widen(tiles[1::2]))]
    )
    zero = jnp.zeros((128, 128), F32)
    return [
        jnp.concatenate(
            [
                jnp.concatenate([tiles[2 * t], zero], axis=1),
                jnp.concatenate([left[t], tiles[2 * t + 1]], axis=1),
            ],
            axis=0,
        )
        for t in range(n_tile)
    ]


def kernel(
    panel_hbm, factor_hbm, rows_hbm, target_ref, out_ref,
    panel, rows, diag, sub, off, vh, vl, oh, ol, fwd, sol, place, send, recv, send_idx, recv_idx,
    load_sem, send_sem, recv_sem,
):
    n_holders = lax.axis_size("row") * lax.axis_size("col")
    me = lax.axis_index("row") * lax.axis_size("col") + lax.axis_index("col")
    n_big = off.shape[0]
    n_tile = diag.shape[0]
    owned = out_ref.shape[0]
    pairs = [(1, 0), (2, 0), (2, 1)]
    loads = []

    def load(src, dst):
        cp = pltpu.make_async_copy(src, dst, load_sem.at[len(loads)])
        cp.start()
        loads.append(cp)
        return cp

    def factor_at(r, c, size):
        return factor_hbm.at[pl.ds(r * size, size), pl.ds(c * size, size)]

    load_diag = [load(factor_at(t, t, TILE), diag.at[t]) for t in range(n_tile)]
    load_sub = [load(factor_at(2 * t + 1, 2 * t, TILE), sub.at[t]) for t in range(n_big)]
    load_off = [load(factor_at(i, j, BIG), off.at[p]) for p, (i, j) in enumerate(pairs)]
    load_panel = load(panel_hbm, panel)
    load_rows = load(rows_hbm, rows)

    barrier = pltpu.get_barrier_semaphore()

    def device_at(o):
        return lax.rem(me + o, n_holders)

    for o in range(1, n_holders):
        pl.semaphore_signal(barrier, inc=1, device_id=device_at(o), device_id_type=LOGICAL)

    sent = target_ref.shape[1]
    target = jnp.broadcast_to(target_ref[...], (8, sent))
    holder = target // owned
    within = target - holder * owned
    lane = iota((8, sent), 1)
    rank = jnp.zeros((8, sent), I32)
    for d in range(1, SLOTS):
        same = (pltpu.roll(holder, d, 1) == holder) & (lane >= d)
        rank = rank + jnp.where(same, 1, 0)
    away = holder - me
    away = jnp.where(away < 0, away + n_holders, away)
    position = (away * SLOTS + rank)[:1]
    slots = n_holders * SLOTS
    placed = jnp.where(iota((slots, sent), 0) == position, 1.0, 0.0).astype(BF16)
    place[...] = placed
    described = jnp.concatenate(
        [jnp.broadcast_to(within[:1].astype(F32), (128, sent)), jnp.ones((128, sent), F32)], axis=0
    ).astype(BF16)
    found = mm_nt(placed, described)
    index = found[:, :128] + EMPTY * (1.0 - found[:, 128:])
    send_idx[...] = index.reshape(n_holders, SLOTS, 128)

    for cp in load_diag:
        cp.wait()
    inverse = invert(diag)
    for b in range(n_big):
        load_sub[b].wait()
        left = split(below(sub[b], inverse[2 * b], inverse[2 * b + 1], TILE))
        top, bottom = split(inverse[2 * b]), split(inverse[2 * b + 1])
        for ref, i in ((vh, 0), (vl, 1)):
            ref[b, :TILE, :TILE] = top[i]
            ref[b, TILE:, TILE:] = bottom[i]
            ref[b, TILE:, :TILE] = left[i]

    for p in range(len(pairs)):
        load_off[p].wait()
        oh[p], ol[p] = split(off[p])

    pl.semaphore_wait(barrier, n_holders - 1)

    def dispatch(source, target_buf, sem_at, offsets):
        for o in offsets:
            if o:
                pltpu.make_async_remote_copy(
                    src_ref=source.at[o],
                    dst_ref=target_buf.at[n_holders - o],
                    send_sem=send_sem.at[sem_at],
                    recv_sem=recv_sem.at[sem_at],
                    device_id=device_at(o),
                    device_id_type=LOGICAL,
                ).start()
            else:
                target_buf[0] = source[0]

    others = pl.ds(1, n_holders - 1)

    def arrived(source, target_buf, sem_at):
        pltpu.make_async_copy(source.at[others], target_buf.at[others], recv_sem.at[sem_at]).wait()

    def left_device(source, target_buf, sem_at):
        pltpu.make_async_copy(source.at[others], target_buf.at[others], send_sem.at[sem_at]).wait()

    dispatch(send_idx, recv_idx, 0, range(n_holders))

    def block_inv(b):
        return (vh[b], vl[b])

    load_panel.wait()
    n_chunk = send.shape[0]
    for ch in range(n_chunk):
        cols = slice(ch * CHUNK, (ch + 1) * CHUNK)
        rhs = [panel[b * BIG : (b + 1) * BIG, cols].astype(F32) for b in range(n_big)]
        for b in range(n_big):
            r = split(rhs[b])
            v = block_inv(b)
            upper = mm3((v[0][:TILE, :TILE], v[1][:TILE, :TILE]), (r[0][:TILE], r[1][:TILE]))
            lower = mm3((v[0][TILE:], v[1][TILE:]), r)
            f = jnp.concatenate([upper, lower], axis=0)
            fwd[:, b * BIG : (b + 1) * BIG] = f.T
            fs = split(f)
            for p, (i, j) in enumerate(pairs):
                if j == b:
                    rhs[i] = rhs[i] - mm3((oh[p], ol[p]), fs)
        for b in reversed(range(n_big)):
            q = split(fwd[:, b * BIG : (b + 1) * BIG])
            v = block_inv(b)
            first = mm3(q, (v[0][:, :TILE], v[1][:, :TILE]))
            second = mm3((q[0][:, TILE:], q[1][:, TILE:]), (v[0][TILE:, TILE:], v[1][TILE:, TILE:]))
            x = jnp.concatenate([first, second], axis=1)
            xs = split(x)
            sol[:, b * BIG : (b + 1) * BIG] = xs[0]
            for p, (i, j) in enumerate(pairs):
                if i == b:
                    at = slice(j * BIG, (j + 1) * BIG)
                    fwd[:, at] = fwd[:, at] - mm3(xs, (oh[p], ol[p]))
        if ch == 0:
            load_rows.wait()
        update = mm_nt(rows[...], sol[...]).astype(BF16)
        step = n_holders // GROUPS
        for g in range(GROUPS):
            some = slice(g * step, (g + 1) * step)
            packed = mm(place[g * step * SLOTS : (g + 1) * step * SLOTS], update).reshape(step, SLOTS, CHUNK)
            send[ch, some] = jnp.concatenate([packed[:, :, :128], packed[:, :, 128:]], axis=1).astype(BF16)
            dispatch(send.at[ch], recv.at[ch], 1 + ch, range(g * step, (g + 1) * step))

    arrived(send_idx, recv_idx, 0)
    pick0 = jnp.where(iota((8, 128), 1) == 0, 1.0, 0.0).astype(BF16)
    named = mm_nt(pick0, recv_idx[...].reshape(slots, 128).astype(BF16))[:1]
    gather = jnp.where(iota((owned, slots), 0).astype(F32) == named, 1.0, 0.0).astype(BF16)
    for ch in range(n_chunk):
        arrived(send.at[ch], recv.at[ch], 1 + ch)
        got = recv[ch].astype(F32)
        got = jnp.concatenate([got[:, :SLOTS].reshape(slots, 128), got[:, SLOTS:].reshape(slots, 128)], axis=1)
        out_ref[:, ch * CHUNK : (ch + 1) * CHUNK] = mm(gather, got.astype(BF16))
    left_device(send_idx, recv_idx, 0)
    for ch in range(n_chunk):
        left_device(send.at[ch], recv.at[ch], 1 + ch)


def local(coupling_panel, interior_factor, border_rows, target_rows, border_block):
    panel, factor, rows = coupling_panel[0], interior_factor[0], border_rows[0]
    n, width = panel.shape
    holders = lax.axis_size("row") * lax.axis_size("col")
    n_tile, n_big, n_chunk = n // TILE, n // BIG, width // CHUNK
    pairs = n_big * (n_big - 1) // 2
    vmem = pl.BlockSpec(memory_space=pltpu.VMEM)
    hbm = pl.BlockSpec(memory_space=pl.ANY)
    assembled = pl.pallas_call(
        kernel,
        out_shape=jax.ShapeDtypeStruct(border_block.shape, F32),
        in_specs=[hbm, hbm, hbm, vmem],
        out_specs=vmem,
        scratch_shapes=[
            pltpu.VMEM(panel.shape, BF16),
            pltpu.VMEM(rows.shape, BF16),
            pltpu.VMEM((n_tile, TILE, TILE), F32),
            pltpu.VMEM((n_big, TILE, TILE), F32),
            pltpu.VMEM((pairs, BIG, BIG), F32),
            pltpu.VMEM((n_big, BIG, BIG), BF16),
            pltpu.VMEM((n_big, BIG, BIG), BF16),
            pltpu.VMEM((pairs, BIG, BIG), BF16),
            pltpu.VMEM((pairs, BIG, BIG), BF16),
            pltpu.VMEM((CHUNK, n), F32),
            pltpu.VMEM((CHUNK, n), BF16),
            pltpu.VMEM((holders * SLOTS, target_rows.shape[1]), BF16),
            pltpu.VMEM((n_chunk, holders, 2 * SLOTS, 128), BF16),
            pltpu.VMEM((n_chunk, holders, 2 * SLOTS, 128), BF16),
            pltpu.VMEM((holders, SLOTS, 128), F32),
            pltpu.VMEM((holders, SLOTS, 128), F32),
            pltpu.SemaphoreType.DMA((n_tile + n_big + pairs + 2,)),
            pltpu.SemaphoreType.DMA((1 + n_chunk,)),
            pltpu.SemaphoreType.DMA((1 + n_chunk,)),
        ],
        compiler_params=pltpu.CompilerParams(
            collective_id=0, has_side_effects=True, vmem_limit_bytes=60 * 1024 * 1024
        ),
        name="schur_panel",
    )(panel, factor, rows, target_rows)
    return border_block - assembled


def solution(mesh):
    placed = (
        P("row", None, None),
        P("row", None, None),
        P("row", "col", None),
        P("row", "col"),
        P(("row", "col"), None),
    )
    return jax.shard_map(
        local, mesh=mesh, in_specs=placed, out_specs=P(("row", "col"), None), check_vma=False
    )
```

time: 50.5 us -> 45.1 us (0.89)
  Pallas kernels: 48.5 us -> 43 us
  other arithmetic: 0 us -> 1.91 us
  local copies, waits for them, and re-layouts: 1.87 us -> 0.01 us
    pallas_call x1, Pallas kernels: 48.5 us -> 43 us  [local(): pl.pallas_call(kernel, out_shape=jax.ShapeDtypeStruct(border_block.shape,...]
    sub x0 -> x1, other arithmetic: none -> 1.91 us  [local(): return border_block - assembled]
    unnamed x1 -> x2, local copies, waits for them, and re-layouts: 1.87 us -> 0.01 us
where the time goes in v2:
time: 45.1 us; the launch traced here: 44.9 us
  Pallas kernels  43 us (95%)
  other arithmetic  1.91 us (4%)
    pallas_call x1, Pallas kernels, local(): pl.pallas_call(kernel, out_shape=jax.ShapeDtypeStruct(border_block.shape,...  43 us
    sub x1, other arithmetic, local(): return border_block - assembled  1.91 us

profile of v2, /device:TPU:1, one launch (start us, length us, event | category | flops | bytes accessed | tf_op | source)
XLA Modules:
  0.0 44.9 jit_solution(14081385328875280123)
XLA Ops:
  0.0 0.0 copy-start
  0.0 43.0 %schur_panel.1 = f32[256,512]{1,0:T(8,128)} custom-call(bf16[1536,512]{1,0:T(8,128)(2,1)} %bitcast.4, f32[1536,1536]{1,0:T(8,128)} %bitcast.3, bf16[512,1536]{1,0:T(8,128)(2,1)} %bitcast.5, s32[1,512]{1,0:T(1,128)} %target_ref.1), custom_call_target="tpu_custom_call" | custom-call | tf_op jit(solution)/shard_map/schur_panel/pallas_call | solution.py:316
  43.0 0.0 copy-done
  43.0 1.9 %sub.3 = f32[256,512]{1,0:T(8,128)} subtract(f32[256,512]{1,0:T(8,128)S(1)} %copy-done, f32[256,512]{1,0:T(8,128)} %schur_panel.1) | non-fusion elementwise | flops 131072 | bytes 1572864 | tf_op jit(solution)/shard_map/sub | solution.py:347
Async XLA Ops:
  0.0 43.0 %copy-start = (f32[256,512]{1,0:T(8,128)S(1)}, f32[256,512]{1,0:T(8,128)}, u32[]{:S(2)}) copy-start(f32[256,512]{1,0:T(8,128)} %param.9) | copy-start | bytes 1572868

commit v3 on v2

v3 whole, which is shorter than its diff:
```python
import jax
import jax.numpy as jnp
from jax import lax
from jax.experimental import pallas as pl
from jax.experimental.pallas import tpu as pltpu
from jax.sharding import PartitionSpec as P

F32, BF16, I32 = jnp.float32, jnp.bfloat16, jnp.int32
BASE = 32
TILE = 256
BIG = 512
CHUNK = 256
SLOTS = 8
GROUPS = 2
LOGICAL = pl.DeviceIdType.LOGICAL
EMPTY = -512.0


def iota(shape, axis):
    return lax.broadcasted_iota(I32, shape, axis)


def split(x):
    hi = x.astype(BF16)
    return hi, (x - hi.astype(F32)).astype(BF16)


def mm(a, b):
    return jnp.dot(a, b, preferred_element_type=F32)


def mm_nt(a, b):
    return lax.dot_general(a, b, (((1,), (1,)), ((), ())), preferred_element_type=F32)


def mm3(a, b):
    return mm(a[0], b[0]) + (mm(a[0], b[1]) + mm(a[1], b[0]))


def invert_base(strip):
    rows, width = strip.shape
    lane = iota((rows, width), 1)
    row = iota((rows, width), 0)
    within = lane % BASE
    start = lane - within
    tiles = range(0, width, 128)
    local = (lane - within)[:, :128] % 128

    def pick(x, index):
        return jnp.concatenate(
            [jnp.take_along_axis(x[:, t : t + 128], index[: x.shape[0]], axis=1) for t in tiles], axis=1
        )

    recip = 1.0 / pick(strip, local + row[:, :128])
    scaled = jnp.where(within < row, strip * recip, 0.0)
    inverse = jnp.where(within == row, recip, 0.0)
    for k in range(rows - 1):
        first = (k + 1) // 8 * 8
        factor = pick(scaled[first:], local + k)
        update = inverse[first:] - factor * inverse[k : k + 1]
        inverse = update if first == 0 else jnp.concatenate([inverse[:first], update], axis=0)
    return inverse


def spread(strip, size):
    if size == TILE:
        return strip
    group = iota((size, TILE), 1) // size
    return tuple(
        jnp.concatenate(
            [part * jnp.where(group == q, 1.0, 0.0).astype(BF16) for q in range(TILE // size)], axis=0
        )
        for part in strip
    )


def below(corner, first, second, size):
    inner = mm3(split(corner), spread(split(first), size))
    return mm3(split(second), spread(split(inner), size))


def widen(tiles):
    return [jnp.concatenate(tiles[t : t + 2], axis=1) for t in range(0, len(tiles), 2)]


def narrow(strips):
    return [w[:, h : h + 128] for w in strips for h in (0, 128)]


def invert(diag):
    n_tile = diag.shape[0]
    small = [
        diag[t, h : h + 128, h : h + 128] for t in range(n_tile) for h in range(0, TILE, 128)
    ]
    group = iota((BASE, 128), 1) // BASE
    strips = []
    for tile in small:
        strip = tile[:BASE]
        for q in range(1, 128 // BASE):
            strip = jnp.where(group == q, tile[q * BASE : (q + 1) * BASE], strip)
        strips.append(strip)
    base = invert_base(jnp.concatenate(strips, axis=1))
    tiles = [base[:, t : t + 128] for t in range(0, base.shape[1], 128)]
    size = BASE
    while size < 128:
        group = iota((size, 128), 1) // size
        even = group % 2 == 0
        corners = []
        for tile in small:
            corner = tile[size : 2 * size]
            for q in range(1, 128 // (2 * size)):
                at = (2 * q + 1) * size
                corner = jnp.where(group == 2 * q, tile[at : at + size], corner)
            corners.append(corner)

        def evens(x):
            return [jnp.where(even, x[t], pltpu.roll(x[t + 1], size, 1)) for t in range(0, len(x), 2)]

        def odds(x):
            return [jnp.where(even, pltpu.roll(x[t], 128 - size, 1), x[t + 1]) for t in range(0, len(x), 2)]

        left = narrow(
            [
                below(c, f, g, size)
                for c, f, g in zip(widen(evens(corners)), widen(evens(tiles)), widen(odds(tiles)))
            ]
        )
        merged = []
        for t, tile in enumerate(tiles):
            x = left[t // 2] if t % 2 == 0 else pltpu.roll(left[t // 2], 128 - size, 1)
            merged.append(
                jnp.concatenate([jnp.where(even, tile, 0.0), jnp.where(even, -x, tile)], axis=0)
            )
        tiles = merged
        size *= 2
    corners = [diag[t, 128:, :128] for t in range(n_tile)]
    left = narrow(
        [below(c, f, g, 128) for c, f, g in zip(widen(corners), widen(tiles[::2]), widen(tiles[1::2]))]
    )
    zero = jnp.zeros((128, 128), F32)
    return [
        jnp.concatenate(
            [
                jnp.concatenate([tiles[2 * t], zero], axis=1),
                jnp.concatenate([-left[t], tiles[2 * t + 1]], axis=1),
            ],
            axis=0,
        )
        for t in range(n_tile)
    ]


def kernel(
    panel_hbm, factor_hbm, rows_hbm, target_ref, out_ref,
    panel, rows, diag, sub, off, vh, vl, oh, ol, fwd, place, send0, recv0, send1, recv1,
    load_sem, send_sem, recv_sem,
):
    n_holders = lax.axis_size("row") * lax.axis_size("col")
    me = lax.axis_index("row") * lax.axis_size("col") + lax.axis_index("col")
    n_big = off.shape[0]
    n_tile = diag.shape[0]
    owned = out_ref.shape[0]
    sends, recvs = (send0, send1), (recv0, recv1)
    pairs = [(1, 0), (2, 0), (2, 1)]
    loads = []

    def load(src, dst):
        cp = pltpu.make_async_copy(src, dst, load_sem.at[len(loads)])
        cp.start()
        loads.append(cp)

    def factor_at(r, c, size):
        return factor_hbm.at[pl.ds(r * size, size), pl.ds(c * size, size)]

    for t in range(n_tile):
        load(factor_at(t, t, TILE), diag.at[t])
    for t in range(n_big):
        load(factor_at(2 * t + 1, 2 * t, TILE), sub.at[t])
    for p, (i, j) in enumerate(pairs):
        load(factor_at(i, j, BIG), off.at[p])
    load(panel_hbm, panel)
    load(rows_hbm, rows)

    with jax.named_scope("greet"):
        barrier = pltpu.get_barrier_semaphore()

        def device_at(o):
            return lax.rem(me + o, n_holders)

        for o in range(1, n_holders):
            pl.semaphore_signal(barrier, inc=1, device_id=device_at(o), device_id_type=LOGICAL)

    for cp in loads[:-2]:
        cp.wait()

    with jax.named_scope("invert"):
        sent = target_ref.shape[1]
        target = jnp.broadcast_to(target_ref[...], (8, sent))
        holder = target // owned
        within = target - holder * owned
        lane = iota((8, sent), 1)
        rank = jnp.zeros((8, sent), I32)
        for d in range(1, SLOTS):
            same = (pltpu.roll(holder, d, 1) == holder) & (lane >= d)
            rank = rank + jnp.where(same, 1, 0)
        away = holder - me
        away = jnp.where(away < 0, away + n_holders, away)
        position = (away * SLOTS + rank)[:1]
        slots = n_holders * SLOTS
        placed = jnp.where(iota((slots, sent), 0) == position, 1.0, 0.0).astype(BF16)
        place[...] = placed
        described = jnp.concatenate(
            [jnp.broadcast_to(within[:1].astype(F32), (128, sent)), jnp.ones((128, sent), F32)], axis=0
        ).astype(BF16)
        found = mm_nt(placed, described)
        index = found[:, :128] + EMPTY * (1.0 - found[:, 128:])
        send0[:, 2 * SLOTS :] = index.reshape(n_holders, SLOTS, 128).astype(BF16)

        inverse = invert(diag)
        for b in range(n_big):
            left = split(below(sub[b], inverse[2 * b], inverse[2 * b + 1], TILE))
            top, bottom = split(inverse[2 * b]), split(inverse[2 * b + 1])
            for ref, i in ((vh, 0), (vl, 1)):
                ref[b, 0] = top[i]
                ref[b, 1] = left[i]
                ref[b, 2] = bottom[i]
        for p in range(len(pairs)):
            oh[p], ol[p] = split(off[p])

    loads[-2].wait()
    loads[-1].wait()
    with jax.named_scope("barwait"):
        pl.semaphore_wait(barrier, n_holders - 1)

    def dispatch(ch):
        for o in range(1, n_holders):
            pltpu.make_async_remote_copy(
                src_ref=sends[ch].at[o],
                dst_ref=recvs[ch].at[n_holders - o],
                send_sem=send_sem.at[ch],
                recv_sem=recv_sem.at[ch],
                device_id=device_at(o),
                device_id_type=LOGICAL,
            ).start()
        recvs[ch][0] = sends[ch][0]

    others = pl.ds(1, n_holders - 1)

    def arrived(ch):
        pltpu.make_async_copy(sends[ch].at[others], recvs[ch].at[others], recv_sem.at[ch]).wait()

    def left_device(ch):
        pltpu.make_async_copy(sends[ch].at[others], recvs[ch].at[others], send_sem.at[ch]).wait()

    def inv(b, part):
        return (vh[b, part], vl[b, part])

    def halves(x, axis):
        if axis == 0:
            return [tuple(y[:TILE] for y in x), tuple(y[TILE:] for y in x)]
        return [tuple(y[:, :TILE] for y in x), tuple(y[:, TILE:] for y in x)]

    n_chunk = len(sends)
    for ch in range(n_chunk):
        with jax.named_scope("fwd"):
            cols = slice(ch * CHUNK, (ch + 1) * CHUNK)
            rhs = [panel[b * BIG : (b + 1) * BIG, cols].astype(F32) for b in range(n_big)]
            for b in range(n_big):
                r = halves(split(rhs[b]), 0)
                upper = mm3(inv(b, 0), r[0])
                lower = mm3(inv(b, 2), r[1]) - mm3(inv(b, 1), r[0])
                f = jnp.concatenate([upper, lower], axis=0)
                fwd[:, b * BIG : (b + 1) * BIG] = f.T
                fs = halves(split(f), 0)
                for p, (i, j) in enumerate(pairs):
                    if j == b:
                        o = halves((oh[p], ol[p]), 1)
                        rhs[i] = (rhs[i] - mm3(o[0], fs[0])) - mm3(o[1], fs[1])
        with jax.named_scope("bwd"):
            partial = []
            for b in reversed(range(n_big)):
                q = halves(split(fwd[:, b * BIG : (b + 1) * BIG]), 1)
                first = mm3(q[0], inv(b, 0)) - mm3(q[1], inv(b, 1))
                second = mm3(q[1], inv(b, 2))
                x = jnp.concatenate([first, second], axis=1)
                xs = halves(split(x), 1)
                for p, (i, j) in reversed(list(enumerate(pairs))):
                    if i == b:
                        at = slice(j * BIG, (j + 1) * BIG)
                        o = halves((oh[p], ol[p]), 0)
                        fwd[:, at] = (fwd[:, at] - mm3(xs[0], o[0])) - mm3(xs[1], o[1])
                at = b * BIG
                if b:
                    partial.append(mm_nt(rows[:, at : at + BIG], jnp.concatenate([-xs[0][0], -xs[1][0]], axis=1)))
                else:
                    update = mm_nt(rows[:, :TILE], xs[0][0]) - mm_nt(rows[:, TILE:BIG], -xs[1][0])
            for other in partial:
                update = update - other
            update = update.astype(BF16)
        with jax.named_scope("pack"):
            step = n_holders // GROUPS
            for g in range(GROUPS):
                some = slice(g * step, (g + 1) * step)
                packed = mm(place[g * step * SLOTS : (g + 1) * step * SLOTS], update).reshape(step, SLOTS, CHUNK)
                packed = jnp.concatenate([packed[:, :, :128], packed[:, :, 128:]], axis=1).astype(BF16)
                sends[ch][some, : 2 * SLOTS] = packed
        with jax.named_scope("send"):
            dispatch(ch)

    for ch in range(n_chunk):
        with jax.named_scope("wait"):
            arrived(ch)
        with jax.named_scope("final"):
            if ch == 0:
                pick0 = jnp.where(iota((8, 128), 1) == 0, 1.0, 0.0).astype(BF16)
                named = mm_nt(pick0, recv0[:, 2 * SLOTS :].astype(F32).reshape(slots, 128).astype(BF16))[:1]
                gather = jnp.where(iota((owned, slots), 0).astype(F32) == named, 1.0, 0.0).astype(BF16)
            got = recvs[ch][:, : 2 * SLOTS].astype(F32)
            got = jnp.concatenate(
                [got[:, :SLOTS].reshape(slots, 128), got[:, SLOTS:].reshape(slots, 128)], axis=1
            )
            out_ref[:, ch * CHUNK : (ch + 1) * CHUNK] = mm(gather, got.astype(BF16))
    for ch in range(n_chunk):
        left_device(ch)


def local(coupling_panel, interior_factor, border_rows, target_rows, border_block):
    panel, factor, rows = coupling_panel[0], interior_factor[0], border_rows[0]
    n, width = panel.shape
    holders = lax.axis_size("row") * lax.axis_size("col")
    n_tile, n_big, n_chunk = n // TILE, n // BIG, width // CHUNK
    pairs = n_big * (n_big - 1) // 2
    vmem = pl.BlockSpec(memory_space=pltpu.VMEM)
    hbm = pl.BlockSpec(memory_space=pl.ANY)
    assembled = pl.pallas_call(
        kernel,
        out_shape=jax.ShapeDtypeStruct(border_block.shape, F32),
        in_specs=[hbm, hbm, hbm, vmem],
        out_specs=vmem,
        scratch_shapes=[
            pltpu.VMEM(panel.shape, BF16),
            pltpu.VMEM(rows.shape, BF16),
            pltpu.VMEM((n_tile, TILE, TILE), F32),
            pltpu.VMEM((n_big, TILE, TILE), F32),
            pltpu.VMEM((pairs, BIG, BIG), F32),
            pltpu.VMEM((n_big, 3, TILE, TILE), BF16),
            pltpu.VMEM((n_big, 3, TILE, TILE), BF16),
            pltpu.VMEM((pairs, BIG, BIG), BF16),
            pltpu.VMEM((pairs, BIG, BIG), BF16),
            pltpu.VMEM((CHUNK, n), F32),
            pltpu.VMEM((holders * SLOTS, target_rows.shape[1]), BF16),
            pltpu.VMEM((holders, 3 * SLOTS, 128), BF16),
            pltpu.VMEM((holders, 3 * SLOTS, 128), BF16),
            pltpu.VMEM((holders, 2 * SLOTS, 128), BF16),
            pltpu.VMEM((holders, 2 * SLOTS, 128), BF16),
            pltpu.SemaphoreType.DMA((n_tile + n_big + pairs + 2,)),
            pltpu.SemaphoreType.DMA((n_chunk,)),
            pltpu.SemaphoreType.DMA((n_chunk,)),
        ],
        compiler_params=pltpu.CompilerParams(
            collective_id=0, has_side_effects=True, vmem_limit_bytes=60 * 1024 * 1024
        ),
        name="schur_panel",
    )(panel, factor, rows, target_rows)
    return border_block - assembled


def solution(mesh):
    placed = (
        P("row", None, None),
        P("row", None, None),
        P("row", "col", None),
        P("row", "col"),
        P(("row", "col"), None),
    )
    return jax.shard_map(
        local, mesh=mesh, in_specs=placed, out_specs=P(("row", "col"), None), check_vma=False
    )
```

time: 45.1 us -> 41.4 us (0.918)
  Pallas kernels: 43 us -> 39.3 us
    pallas_call x1, Pallas kernels: 43 us -> 39.3 us  [local(): pl.pallas_call(kernel, out_shape=jax.ShapeDtypeStruct(border_block.shape,...]
where the time goes in v3:
time: 41.4 us; the launch traced here: 41.2 us
  Pallas kernels  39.3 us (95%)
  other arithmetic  1.91 us (5%)
    pallas_call x1, Pallas kernels, local(): pl.pallas_call(kernel, out_shape=jax.ShapeDtypeStruct(border_block.shape,...  39.3 us
    sub x1, other arithmetic, local(): return border_block - assembled  1.91 us

profile of v3, /device:TPU:1, one launch (start us, length us, event | category | flops | bytes accessed | tf_op | source)
XLA Modules:
  0.0 41.2 jit_solution(7063523750726706799)
XLA Ops:
  0.0 0.0 copy-start
  0.0 39.3 %schur_panel.1 = f32[256,512]{1,0:T(8,128)} custom-call(bf16[1536,512]{1,0:T(8,128)(2,1)} %bitcast.4, f32[1536,1536]{1,0:T(8,128)} %bitcast.3, bf16[512,1536]{1,0:T(8,128)(2,1)} %bitcast.5, s32[1,512]{1,0:T(1,128)} %target_ref.1), custom_call_target="tpu_custom_call" | custom-call | tf_op jit(solution)/shard_map/schur_panel/pallas_call | solution.py:335
  39.3 0.0 copy-done
  39.3 1.9 %sub.3 = f32[256,512]{1,0:T(8,128)} subtract(f32[256,512]{1,0:T(8,128)S(1)} %copy-done, f32[256,512]{1,0:T(8,128)} %schur_panel.1) | non-fusion elementwise | flops 131072 | bytes 1572864 | tf_op jit(solution)/shard_map/sub | solution.py:365
Async XLA Ops:
  0.0 39.3 %copy-start = (f32[256,512]{1,0:T(8,128)S(1)}, f32[256,512]{1,0:T(8,128)}, u32[]{:S(2)}) copy-start(f32[256,512]{1,0:T(8,128)} %param.9) | copy-start | bytes 1572868

commit v4 on v3

--- a/solution.py
+++ b/solution.py
@@ -6,12 +6,14 @@
 from jax.sharding import PartitionSpec as P
 
 F32, BF16, I32 = jnp.float32, jnp.bfloat16, jnp.int32
-BASE = 32
+BASE = 16
 TILE = 256
 BIG = 512
 CHUNK = 256
 SLOTS = 8
 GROUPS = 2
+SIDE = 4
+CORES = 2
 LOGICAL = pl.DeviceIdType.LOGICAL
 EMPTY = -512.0
 
@@ -87,11 +89,12 @@
     return [w[:, h : h + 128] for w in strips for h in (0, 128)]
 
 
-def invert(diag):
-    n_tile = diag.shape[0]
-    small = [
-        diag[t, h : h + 128, h : h + 128] for t in range(n_tile) for h in range(0, TILE, 128)
-    ]
+def small_tiles(diag):
+    return [diag[t, h : h + 128, h : h + 128] for t in range(diag.shape[0]) for h in range(0, TILE, 128)]
+
+
+def invert_bases(diag):
+    small = small_tiles(diag)
     group = iota((BASE, 128), 1) // BASE
     strips = []
     for tile in small:
@@ -100,7 +103,12 @@
             strip = jnp.where(group == q, tile[q * BASE : (q + 1) * BASE], strip)
         strips.append(strip)
     base = invert_base(jnp.concatenate(strips, axis=1))
-    tiles = [base[:, t : t + 128] for t in range(0, base.shape[1], 128)]
+    return [base[:, t : t + 128] for t in range(0, base.shape[1], 128)]
+
+
+def invert(diag, tiles):
+    n_tile = diag.shape[0]
+    small = small_tiles(diag)
     size = BASE
     while size < 128:
         group = iota((size, 128), 1) // size
@@ -150,18 +158,62 @@
     ]
 
 
+def parts_of(device):
+    col = SIDE * SIDE
+    return (
+        lax.div(device, CORES * col),
+        lax.rem(lax.div(device, col), CORES),
+        lax.rem(lax.div(device, SIDE), SIDE),
+        lax.rem(device, SIDE),
+    )
+
+
+def joined(y, core, x, z):
+    return ((y * CORES + core) * SIDE + x) * SIDE + z
+
+
+SIZES = (SIDE, CORES, SIDE, SIDE)
+
+
+def steps_of(offset):
+    return (
+        offset // (CORES * SIDE * SIDE),
+        offset // (SIDE * SIDE) % CORES,
+        offset // SIDE % SIDE,
+        offset % SIDE,
+    )
+
+
+def opposite(offset):
+    return joined(*((n - d) % n for n, d in zip(SIZES, steps_of(offset))))
+
+
+def hops(offset):
+    y, core, x, z = steps_of(offset)
+    return sum(min(d, SIDE - d) for d in (y, x, z)) + 0.5 * core
+
+
 def kernel(
-    panel_hbm, factor_hbm, rows_hbm, target_ref, out_ref,
-    panel, rows, diag, sub, off, vh, vl, oh, ol, fwd, place, send0, recv0, send1, recv1,
+    panel_hbm, factor_hbm, rows_hbm, target_hbm, out_ref,
+    panel, rows, diag, sub, off, vh, vl, oh, ol, fwd, place, send0, recv0, send1, recv1, target_ref, result,
     load_sem, send_sem, recv_sem,
 ):
     n_holders = lax.axis_size("row") * lax.axis_size("col")
     me = lax.axis_index("row") * lax.axis_size("col") + lax.axis_index("col")
+    here = parts_of(me)
     n_big = off.shape[0]
     n_tile = diag.shape[0]
-    owned = out_ref.shape[0]
+    owned = result.shape[0]
     sends, recvs = (send0, send1), (recv0, recv1)
     pairs = [(1, 0), (2, 0), (2, 1)]
+    offsets = sorted(range(1, n_holders), key=lambda o: -hops(o))
+    ahead = [[lax.rem(c + d, n) for d in range(n)] for c, n in zip(here, SIZES)]
+    rows_ahead = [joined(y, core, 0, 0) for y in ahead[0] for core in ahead[1]]
+    cols_ahead = [joined(0, 0, x, z) for x in ahead[2] for z in ahead[3]]
+
+    def device_at(o):
+        return rows_ahead[o // (SIDE * SIDE)] + cols_ahead[o % (SIDE * SIDE)]
+
     loads = []
 
     def load(src, dst):
@@ -178,19 +230,20 @@
         load(factor_at(2 * t + 1, 2 * t, TILE), sub.at[t])
     for p, (i, j) in enumerate(pairs):
         load(factor_at(i, j, BIG), off.at[p])
+    load(target_hbm, target_ref)
     load(panel_hbm, panel)
     load(rows_hbm, rows)
 
     with jax.named_scope("greet"):
         barrier = pltpu.get_barrier_semaphore()
-
-        def device_at(o):
-            return lax.rem(me + o, n_holders)
-
-        for o in range(1, n_holders):
+        for o in offsets:
             pl.semaphore_signal(barrier, inc=1, device_id=device_at(o), device_id_type=LOGICAL)
 
-    for cp in loads[:-2]:
+    for cp in loads[:n_tile]:
+        cp.wait()
+    with jax.named_scope("base"):
+        base = invert_bases(diag)
+    for cp in loads[n_tile:-2]:
         cp.wait()
 
     with jax.named_scope("invert"):
@@ -203,8 +256,7 @@
         for d in range(1, SLOTS):
             same = (pltpu.roll(holder, d, 1) == holder) & (lane >= d)
             rank = rank + jnp.where(same, 1, 0)
-        away = holder - me
-        away = jnp.where(away < 0, away + n_holders, away)
+        away = joined(*(lax.rem(h - c + n, n) for h, c, n in zip(parts_of(holder), here, SIZES)))
         position = (away * SLOTS + rank)[:1]
         slots = n_holders * SLOTS
         placed = jnp.where(iota((slots, sent), 0) == position, 1.0, 0.0).astype(BF16)
@@ -216,7 +268,7 @@
         index = found[:, :128] + EMPTY * (1.0 - found[:, 128:])
         send0[:, 2 * SLOTS :] = index.reshape(n_holders, SLOTS, 128).astype(BF16)
 
-        inverse = invert(diag)
+        inverse = invert(diag, base)
         for b in range(n_big):
             left = split(below(sub[b], inverse[2 * b], inverse[2 * b + 1], TILE))
             top, bottom = split(inverse[2 * b]), split(inverse[2 * b + 1])
@@ -233,10 +285,10 @@
         pl.semaphore_wait(barrier, n_holders - 1)
 
     def dispatch(ch):
-        for o in range(1, n_holders):
+        for o in offsets:
             pltpu.make_async_remote_copy(
                 src_ref=sends[ch].at[o],
-                dst_ref=recvs[ch].at[n_holders - o],
+                dst_ref=recvs[ch].at[opposite(o)],
                 send_sem=send_sem.at[ch],
                 recv_sem=recv_sem.at[ch],
                 device_id=device_at(o),
@@ -307,6 +359,7 @@
         with jax.named_scope("send"):
             dispatch(ch)
 
+    stores = []
     for ch in range(n_chunk):
         with jax.named_scope("wait"):
             arrived(ch)
@@ -319,9 +372,14 @@
             got = jnp.concatenate(
                 [got[:, :SLOTS].reshape(slots, 128), got[:, SLOTS:].reshape(slots, 128)], axis=1
             )
-            out_ref[:, ch * CHUNK : (ch + 1) * CHUNK] = mm(gather, got.astype(BF16))
+            cols = pl.ds(ch * CHUNK, CHUNK)
+            result[:, cols] = mm(gather, got.astype(BF16))
+        store = pltpu.make_async_copy(result.at[:, cols], out_ref.at[:, cols], load_sem.at[ch])
+        store.start()
+        stores.append(store)
     for ch in range(n_chunk):
         left_device(ch)
+        stores[ch].wait()
 
 
 def local(coupling_panel, interior_factor, border_rows, target_rows, border_block):
@@ -330,13 +388,12 @@
     holders = lax.axis_size("row") * lax.axis_size("col")
     n_tile, n_big, n_chunk = n // TILE, n // BIG, width // CHUNK
     pairs = n_big * (n_big - 1) // 2
-    vmem = pl.BlockSpec(memory_space=pltpu.VMEM)
     hbm = pl.BlockSpec(memory_space=pl.ANY)
     assembled = pl.pallas_call(
         kernel,
         out_shape=jax.ShapeDtypeStruct(border_block.shape, F32),
-        in_specs=[hbm, hbm, hbm, vmem],
-        out_specs=vmem,
+        in_specs=[hbm] * 4,
+        out_specs=hbm,
         scratch_shapes=[
             pltpu.VMEM(panel.shape, BF16),
             pltpu.VMEM(rows.shape, BF16),
@@ -353,12 +410,14 @@
             pltpu.VMEM((holders, 3 * SLOTS, 128), BF16),
             pltpu.VMEM((holders, 2 * SLOTS, 128), BF16),
             pltpu.VMEM((holders, 2 * SLOTS, 128), BF16),
-            pltpu.SemaphoreType.DMA((n_tile + n_big + pairs + 2,)),
+            pltpu.VMEM(target_rows.shape, I32),
+            pltpu.VMEM(border_block.shape, F32),
+            pltpu.SemaphoreType.DMA((n_tile + n_big + pairs + 3,)),
             pltpu.SemaphoreType.DMA((n_chunk,)),
             pltpu.SemaphoreType.DMA((n_chunk,)),
         ],
         compiler_params=pltpu.CompilerParams(
-            collective_id=0, has_side_effects=True, vmem_limit_bytes=60 * 1024 * 1024
+            collective_id=0, has_side_effects=True, vmem_limit_bytes=53 * 1024 * 1024
         ),
         name="schur_panel",
     )(panel, factor, rows, target_rows)

time: 41.4 us -> 37.3 us (0.901)
  Pallas kernels: 39.3 us -> 35.5 us
  other arithmetic: 1.91 us -> 0.87 us
  local copies, waits for them, and re-layouts: 0.01 us -> 0.68 us
    pallas_call x1, Pallas kernels: 39.3 us -> 35.5 us  [local(): pl.pallas_call(kernel, out_shape=jax.ShapeDtypeStruct(border_block.shape,...]
    sub x1, other arithmetic: 1.91 us -> 0.87 us  [local(): return border_block - assembled]
    unnamed x2 -> x4, local copies, waits for them, and re-layouts: 0.01 us -> 0.68 us
where the time goes in v4:
time: 37.3 us; the launch traced here: 37.1 us
  Pallas kernels  35.5 us (95%)
  other arithmetic  0.87 us (2%)
  local copies, waits for them, and re-layouts  0.68 us (2%)
    pallas_call x1, Pallas kernels, local(): pl.pallas_call(kernel, out_shape=jax.ShapeDtypeStruct(border_block.shape,...  35.5 us
    sub x1, other arithmetic, local(): return border_block - assembled  0.87 us

profile of v4, /device:TPU:1, one launch (start us, length us, event | category | flops | bytes accessed | tf_op | source)
XLA Modules:
  0.0 37.1 jit_solution(15810560559818223468)
XLA Ops:
  0.0 0.0 copy-start
  0.0 0.7 %copy-done = s32[1,512]{1,0:T(1,128)S(1)} copy-done((s32[1,512]{1,0:T(1,128)S(1)}, s32[1,512]{1,0:T(1,128)}, u32[]{:S(2)}) %copy-start) | copy-done | bytes 2072
  0.7 0.0 copy-start.1
  0.7 35.5 %schur_panel.1 = f32[256,512]{1,0:T(8,128)S(1)} custom-call(bf16[1536,512]{1,0:T(8,128)(2,1)} %bitcast.4, f32[1536,1536]{1,0:T(8,128)} %bitcast.3, bf16[512,1536]{1,0:T(8,128)(2,1)} %bitcast.5, s32[1,512]{1,0:T(1,128)S(1)} %copy-done), custom_call_target="tpu_custom_call" | custom-call | tf_op jit(solution)/shard_map/schur_panel/pallas_call | solution.py:392
  36.2 0.0 copy-done.1
  36.2 0.9 %sub.3 = f32[256,512]{1,0:T(8,128)} subtract(f32[256,512]{1,0:T(8,128)S(1)} %copy-done.1, f32[256,512]{1,0:T(8,128)S(1)} %schur_panel.1) | non-fusion elementwise | flops 131072 | bytes 1572864 | tf_op jit(solution)/shard_map/sub | solution.py:424
Async XLA Ops:
  0.0 0.7 %copy-start = (s32[1,512]{1,0:T(1,128)S(1)}, s32[1,512]{1,0:T(1,128)}, u32[]{:S(2)}) copy-start(s32[1,512]{1,0:T(1,128)} %target_hbm.1) | copy-start | bytes 6148
  0.7 35.5 %copy-start.1 = (f32[256,512]{1,0:T(8,128)S(1)}, f32[256,512]{1,0:T(8,128)}, u32[]{:S(2)}) copy-start(f32[256,512]{1,0:T(8,128)} %param.9) | copy-start | bytes 1572868

commit v5 on v4

--- a/solution.py
+++ b/solution.py
@@ -90,7 +90,7 @@
 
 
 def small_tiles(diag):
-    return [diag[t, h : h + 128, h : h + 128] for t in range(diag.shape[0]) for h in range(0, TILE, 128)]
+    return [diag[t, h] for t in range(diag.shape[0]) for h in range(2)]
 
 
 def invert_bases(diag):
@@ -106,8 +106,7 @@
     return [base[:, t : t + 128] for t in range(0, base.shape[1], 128)]
 
 
-def invert(diag, tiles):
-    n_tile = diag.shape[0]
+def invert_small(diag, tiles):
     small = small_tiles(diag)
     size = BASE
     while size < 128:
@@ -141,7 +140,12 @@
             )
         tiles = merged
         size *= 2
-    corners = [diag[t, 128:, :128] for t in range(n_tile)]
+    return tiles
+
+
+def invert_tiles(diag, tiles):
+    n_tile = diag.shape[0]
+    corners = [diag[t, 2] for t in range(n_tile)]
     left = narrow(
         [below(c, f, g, 128) for c, f, g in zip(widen(corners), widen(tiles[::2]), widen(tiles[1::2]))]
     )
@@ -224,13 +228,16 @@
     def factor_at(r, c, size):
         return factor_hbm.at[pl.ds(r * size, size), pl.ds(c * size, size)]
 
+    load(target_hbm, target_ref)
     for t in range(n_tile):
-        load(factor_at(t, t, TILE), diag.at[t])
+        load(factor_at(2 * t, 2 * t, 128), diag.at[t, 0])
+        load(factor_at(2 * t + 1, 2 * t + 1, 128), diag.at[t, 1])
+    for t in range(n_tile):
+        load(factor_at(2 * t + 1, 2 * t, 128), diag.at[t, 2])
     for t in range(n_big):
         load(factor_at(2 * t + 1, 2 * t, TILE), sub.at[t])
     for p, (i, j) in enumerate(pairs):
         load(factor_at(i, j, BIG), off.at[p])
-    load(target_hbm, target_ref)
     load(panel_hbm, panel)
     load(rows_hbm, rows)
 
@@ -239,14 +246,10 @@
         for o in offsets:
             pl.semaphore_signal(barrier, inc=1, device_id=device_at(o), device_id_type=LOGICAL)
 
-    for cp in loads[:n_tile]:
+    first, second = 2 * n_tile + 1, 3 * n_tile + n_big + 1
+    for cp in loads[:first]:
         cp.wait()
-    with jax.named_scope("base"):
-        base = invert_bases(diag)
-    for cp in loads[n_tile:-2]:
-        cp.wait()
-
-    with jax.named_scope("invert"):
+    with jax.named_scope("place"):
         sent = target_ref.shape[1]
         target = jnp.broadcast_to(target_ref[...], (8, sent))
         holder = target // owned
@@ -267,8 +270,12 @@
         found = mm_nt(placed, described)
         index = found[:, :128] + EMPTY * (1.0 - found[:, 128:])
         send0[:, 2 * SLOTS :] = index.reshape(n_holders, SLOTS, 128).astype(BF16)
-
-        inverse = invert(diag, base)
+    with jax.named_scope("small"):
+        small = invert_small(diag, invert_bases(diag))
+    for cp in loads[first:second]:
+        cp.wait()
+    with jax.named_scope("merge"):
+        inverse = invert_tiles(diag, small)
         for b in range(n_big):
             left = split(below(sub[b], inverse[2 * b], inverse[2 * b + 1], TILE))
             top, bottom = split(inverse[2 * b]), split(inverse[2 * b + 1])
@@ -276,14 +283,11 @@
                 ref[b, 0] = top[i]
                 ref[b, 1] = left[i]
                 ref[b, 2] = bottom[i]
+    for cp in loads[second:]:
+        cp.wait()
+    with jax.named_scope("split"):
         for p in range(len(pairs)):
             oh[p], ol[p] = split(off[p])
-
-    loads[-2].wait()
-    loads[-1].wait()
-    with jax.named_scope("barwait"):
-        pl.semaphore_wait(barrier, n_holders - 1)
-
     def dispatch(ch):
         for o in offsets:
             pltpu.make_async_remote_copy(
@@ -357,6 +361,8 @@
                 packed = jnp.concatenate([packed[:, :, :128], packed[:, :, 128:]], axis=1).astype(BF16)
                 sends[ch][some, : 2 * SLOTS] = packed
         with jax.named_scope("send"):
+            if ch == 0:
+                pl.semaphore_wait(barrier, n_holders - 1)
             dispatch(ch)
 
     stores = []
@@ -397,7 +403,7 @@
         scratch_shapes=[
             pltpu.VMEM(panel.shape, BF16),
             pltpu.VMEM(rows.shape, BF16),
-            pltpu.VMEM((n_tile, TILE, TILE), F32),
+            pltpu.VMEM((n_tile, 3, 128, 128), F32),
             pltpu.VMEM((n_big, TILE, TILE), F32),
             pltpu.VMEM((pairs, BIG, BIG), F32),
             pltpu.VMEM((n_big, 3, TILE, TILE), BF16),
@@ -412,7 +418,7 @@
             pltpu.VMEM((holders, 2 * SLOTS, 128), BF16),
             pltpu.VMEM(target_rows.shape, I32),
             pltpu.VMEM(border_block.shape, F32),
-            pltpu.SemaphoreType.DMA((n_tile + n_big + pairs + 3,)),
+            pltpu.SemaphoreType.DMA((3 * n_tile + n_big + pairs + 3,)),
             pltpu.SemaphoreType.DMA((n_chunk,)),
             pltpu.SemaphoreType.DMA((n_chunk,)),
         ],

time: 37.3 us -> 36.3 us (0.973)
  Pallas kernels: 35.5 us -> 34.5 us
    pallas_call x1, Pallas kernels: 35.5 us -> 34.5 us  [local(): pl.pallas_call(kernel, out_shape=jax.ShapeDtypeStruct(border_block.shape,...]
where the time goes in v5:
time: 36.3 us; the launch traced here: 36 us
  Pallas kernels  34.5 us (95%)
  other arithmetic  0.87 us (2%)
  local copies, waits for them, and re-layouts  0.68 us (2%)
    pallas_call x1, Pallas kernels, local(): pl.pallas_call(kernel, out_shape=jax.ShapeDtypeStruct(border_block.shape,...  34.5 us
    sub x1, other arithmetic, local(): return border_block - assembled  0.87 us

profile of v5, /device:TPU:1, one launch (start us, length us, event | category | flops | bytes accessed | tf_op | source)
XLA Modules:
  0.0 36.0 jit_solution(15652175554631818185)
XLA Ops:
  0.0 0.0 copy-start
  0.0 0.7 %copy-done = s32[1,512]{1,0:T(1,128)S(1)} copy-done((s32[1,512]{1,0:T(1,128)S(1)}, s32[1,512]{1,0:T(1,128)}, u32[]{:S(2)}) %copy-start) | copy-done | bytes 2072
  0.7 0.0 copy-start.1
  0.7 34.5 %schur_panel.1 = f32[256,512]{1,0:T(8,128)S(1)} custom-call(bf16[1536,512]{1,0:T(8,128)(2,1)} %bitcast.4, f32[1536,1536]{1,0:T(8,128)} %bitcast.3, bf16[512,1536]{1,0:T(8,128)(2,1)} %bitcast.5, s32[1,512]{1,0:T(1,128)S(1)} %copy-done), custom_call_target="tpu_custom_call" | custom-call | tf_op jit(solution)/shard_map/schur_panel/pallas_call | solution.py:398
  35.2 0.0 copy-done.1
  35.2 0.9 %sub.3 = f32[256,512]{1,0:T(8,128)} subtract(f32[256,512]{1,0:T(8,128)S(1)} %copy-done.1, f32[256,512]{1,0:T(8,128)S(1)} %schur_panel.1) | non-fusion elementwise | flops 131072 | bytes 1572864 | tf_op jit(solution)/shard_map/sub | solution.py:430
Async XLA Ops:
  0.0 0.7 %copy-start = (s32[1,512]{1,0:T(1,128)S(1)}, s32[1,512]{1,0:T(1,128)}, u32[]{:S(2)}) copy-start(s32[1,512]{1,0:T(1,128)} %target_hbm.1) | copy-start | bytes 6148
  0.7 34.5 %copy-start.1 = (f32[256,512]{1,0:T(8,128)S(1)}, f32[256,512]{1,0:T(8,128)}, u32[]{:S(2)}) copy-start(f32[256,512]{1,0:T(8,128)} %param.9) | copy-start | bytes 1572868

commit v6 on v5

--- a/solution.py
+++ b/solution.py
@@ -64,29 +64,28 @@
     return inverse
 
 
+def stacked(a, b):
+    rows = a[0].shape[0]
+    both = mm(jnp.concatenate(a, axis=0), b[0])
+    return both[:rows] + (both[rows:] + mm(a[0], b[1]))
+
+
 def spread(strip, size):
-    if size == TILE:
+    width = strip[0].shape[1]
+    if size == width:
         return strip
-    group = iota((size, TILE), 1) // size
+    group = iota((size, width), 1) // size
     return tuple(
         jnp.concatenate(
-            [part * jnp.where(group == q, 1.0, 0.0).astype(BF16) for q in range(TILE // size)], axis=0
+            [part * jnp.where(group == q, 1.0, 0.0).astype(BF16) for q in range(width // size)], axis=0
         )
         for part in strip
     )
 
 
 def below(corner, first, second, size):
-    inner = mm3(split(corner), spread(split(first), size))
-    return mm3(split(second), spread(split(inner), size))
-
-
-def widen(tiles):
-    return [jnp.concatenate(tiles[t : t + 2], axis=1) for t in range(0, len(tiles), 2)]
-
-
-def narrow(strips):
-    return [w[:, h : h + 128] for w in strips for h in (0, 128)]
+    inner = stacked(split(corner), spread(split(first), size))
+    return stacked(split(second), spread(split(inner), size))
 
 
 def small_tiles(diag):
@@ -126,12 +125,7 @@
         def odds(x):
             return [jnp.where(even, pltpu.roll(x[t], 128 - size, 1), x[t + 1]) for t in range(0, len(x), 2)]
 
-        left = narrow(
-            [
-                below(c, f, g, size)
-                for c, f, g in zip(widen(evens(corners)), widen(evens(tiles)), widen(odds(tiles)))
-            ]
-        )
+        left = [below(c, f, g, size) for c, f, g in zip(evens(corners), evens(tiles), odds(tiles))]
         merged = []
         for t, tile in enumerate(tiles):
             x = left[t // 2] if t % 2 == 0 else pltpu.roll(left[t // 2], 128 - size, 1)
@@ -145,10 +139,7 @@
 
 def invert_tiles(diag, tiles):
     n_tile = diag.shape[0]
-    corners = [diag[t, 2] for t in range(n_tile)]
-    left = narrow(
-        [below(c, f, g, 128) for c, f, g in zip(widen(corners), widen(tiles[::2]), widen(tiles[1::2]))]
-    )
+    left = [below(diag[t, 2], tiles[2 * t], tiles[2 * t + 1], 128) for t in range(n_tile)]
     zero = jnp.zeros((128, 128), F32)
     return [
         jnp.concatenate(
@@ -195,6 +186,16 @@
 def hops(offset):
     y, core, x, z = steps_of(offset)
     return sum(min(d, SIDE - d) for d in (y, x, z)) + 0.5 * core
+
+
+def send_order(n):
+    classes = {}
+    for o in sorted(range(1, n), key=lambda o: -hops(o)):
+        y, core, x, z = steps_of(o)
+        moved = ("x", x) if x else ("y", y) if y else ("z", z)
+        classes.setdefault(moved, []).append(o)
+    placed = [((i + 0.5) / len(c), -len(c), o) for c in classes.values() for i, o in enumerate(c)]
+    return [o for _, _, o in sorted(placed)]
 
 
 def kernel(
@@ -210,7 +211,7 @@
     owned = result.shape[0]
     sends, recvs = (send0, send1), (recv0, recv1)
     pairs = [(1, 0), (2, 0), (2, 1)]
-    offsets = sorted(range(1, n_holders), key=lambda o: -hops(o))
+    offsets = send_order(n_holders)
     ahead = [[lax.rem(c + d, n) for d in range(n)] for c, n in zip(here, SIZES)]
     rows_ahead = [joined(y, core, 0, 0) for y in ahead[0] for core in ahead[1]]
     cols_ahead = [joined(0, 0, x, z) for x in ahead[2] for z in ahead[3]]

time: 36.3 us -> 36.1 us (level)
  Pallas kernels: 34.5 us -> 34.1 us
    pallas_call x1, Pallas kernels: 34.5 us -> 34.1 us  [local(): pl.pallas_call(kernel, out_shape=jax.ShapeDtypeStruct(border_block.shape,...]
where the time goes in v6:
time: 36.1 us; the launch traced here: 35.6 us
  Pallas kernels  34.1 us (94%)
  other arithmetic  0.87 us (2%)
  local copies, waits for them, and re-layouts  0.68 us (2%)
    pallas_call x1, Pallas kernels, local(): pl.pallas_call(kernel, out_shape=jax.ShapeDtypeStruct(border_block.shape,...  34.1 us
    sub x1, other arithmetic, local(): return border_block - assembled  0.87 us

profile of v6, /device:TPU:1, one launch (start us, length us, event | category | flops | bytes accessed | tf_op | source)
XLA Modules:
  0.0 35.6 jit_solution(13222320318992360581)
XLA Ops:
  0.0 0.0 copy-start
  0.0 0.7 %copy-done = s32[1,512]{1,0:T(1,128)S(1)} copy-done((s32[1,512]{1,0:T(1,128)S(1)}, s32[1,512]{1,0:T(1,128)}, u32[]{:S(2)}) %copy-start) | copy-done | bytes 2072
  0.7 0.0 copy-start.1
  0.7 34.1 %schur_panel.1 = f32[256,512]{1,0:T(8,128)S(1)} custom-call(bf16[1536,512]{1,0:T(8,128)(2,1)} %bitcast.4, f32[1536,1536]{1,0:T(8,128)} %bitcast.3, bf16[512,1536]{1,0:T(8,128)(2,1)} %bitcast.5, s32[1,512]{1,0:T(1,128)S(1)} %copy-done), custom_call_target="tpu_custom_call" | custom-call | tf_op jit(solution)/shard_map/schur_panel/pallas_call | solution.py:399
  34.8 0.0 copy-done.1
  34.8 0.9 %sub.3 = f32[256,512]{1,0:T(8,128)} subtract(f32[256,512]{1,0:T(8,128)S(1)} %copy-done.1, f32[256,512]{1,0:T(8,128)S(1)} %schur_panel.1) | non-fusion elementwise | flops 131072 | bytes 1572864 | tf_op jit(solution)/shard_map/sub | solution.py:431
Async XLA Ops:
  0.0 0.7 %copy-start = (s32[1,512]{1,0:T(1,128)S(1)}, s32[1,512]{1,0:T(1,128)}, u32[]{:S(2)}) copy-start(s32[1,512]{1,0:T(1,128)} %target_hbm.1) | copy-start | bytes 6148
  0.7 34.1 %copy-start.1 = (f32[256,512]{1,0:T(8,128)S(1)}, f32[256,512]{1,0:T(8,128)}, u32[]{:S(2)}) copy-start(f32[256,512]{1,0:T(8,128)} %param.9) | copy-start | bytes 1572868

commit v7 on v6

--- a/solution.py
+++ b/solution.py
@@ -105,10 +105,11 @@
     return [base[:, t : t + 128] for t in range(0, base.shape[1], 128)]
 
 
-def invert_small(diag, tiles):
+def invert_small(diag, tiles, between):
     small = small_tiles(diag)
     size = BASE
     while size < 128:
+        between()
         group = iota((size, 128), 1) // size
         even = group % 2 == 0
         corners = []
@@ -200,16 +201,20 @@
 
 def kernel(
     panel_hbm, factor_hbm, rows_hbm, target_hbm, out_ref,
-    panel, rows, diag, sub, off, vh, vl, oh, ol, fwd, place, send0, recv0, send1, recv1, target_ref, result,
+    panel, rows, diag, sub, off, vh, vl, oh, ol, fwd, place, send0, recv0, send1, recv1,
+    row_send, row_recv, col_recv, target_ref, result,
     load_sem, send_sem, recv_sem,
 ):
     n_holders = lax.axis_size("row") * lax.axis_size("col")
     me = lax.axis_index("row") * lax.axis_size("col") + lax.axis_index("col")
     here = parts_of(me)
+    n_col = SIDE * SIDE
+    n_row = n_holders // n_col
     n_big = off.shape[0]
     n_tile = diag.shape[0]
     owned = result.shape[0]
     sends, recvs = (send0, send1), (recv0, recv1)
+    n_chunk = len(sends)
     pairs = [(1, 0), (2, 0), (2, 1)]
     offsets = send_order(n_holders)
     ahead = [[lax.rem(c + d, n) for d in range(n)] for c, n in zip(here, SIZES)]
@@ -242,14 +247,25 @@
     load(panel_hbm, panel)
     load(rows_hbm, rows)
 
-    with jax.named_scope("greet"):
-        barrier = pltpu.get_barrier_semaphore()
-        for o in offsets:
-            pl.semaphore_signal(barrier, inc=1, device_id=device_at(o), device_id_type=LOGICAL)
+    barrier = pltpu.get_barrier_semaphore()
+
+    @pl.when(me != 0)
+    def _():
+        pl.semaphore_signal(barrier, inc=1, device_id=0, device_id_type=LOGICAL)
+
+    def all_entered():
+        @pl.when(me == 0)
+        def _():
+            pl.semaphore_wait(barrier, n_holders - 1)
+            for o in range(1, n_holders):
+                pl.semaphore_signal(barrier, inc=1, device_id=o, device_id_type=LOGICAL)
+
+        @pl.when(me != 0)
+        def _():
+            pl.semaphore_wait(barrier, 1)
 
     first, second = 2 * n_tile + 1, 3 * n_tile + n_big + 1
-    for cp in loads[:first]:
-        cp.wait()
+    loads[0].wait()
     with jax.named_scope("place"):
         sent = target_ref.shape[1]
         target = jnp.broadcast_to(target_ref[...], (8, sent))
@@ -270,10 +286,19 @@
         ).astype(BF16)
         found = mm_nt(placed, described)
         index = found[:, :128] + EMPTY * (1.0 - found[:, 128:])
-        send0[:, 2 * SLOTS :] = index.reshape(n_holders, SLOTS, 128).astype(BF16)
+        index = index.reshape(n_row, n_col, SLOTS, 128).astype(BF16)
+        for c in range(n_col):
+            row_send[c] = index[:, c]
+    for cp in loads[1:first]:
+        cp.wait()
+    waiting = loads[first:second]
+
+    def between():
+        waiting.pop(0).wait()
+
     with jax.named_scope("small"):
-        small = invert_small(diag, invert_bases(diag))
-    for cp in loads[first:second]:
+        small = invert_small(diag, invert_bases(diag), between)
+    for cp in waiting:
         cp.wait()
     with jax.named_scope("merge"):
         inverse = invert_tiles(diag, small)
@@ -286,9 +311,6 @@
                 ref[b, 2] = bottom[i]
     for cp in loads[second:]:
         cp.wait()
-    with jax.named_scope("split"):
-        for p in range(len(pairs)):
-            oh[p], ol[p] = split(off[p])
     def dispatch(ch):
         for o in offsets:
             pltpu.make_async_remote_copy(
@@ -309,6 +331,31 @@
     def left_device(ch):
         pltpu.make_async_copy(sends[ch].at[others], recvs[ch].at[others], send_sem.at[ch]).wait()
 
+    def start(src, dst, o, at):
+        pltpu.make_async_remote_copy(
+            src_ref=src, dst_ref=dst, send_sem=send_sem.at[at], recv_sem=recv_sem.at[at],
+            device_id=device_at(o), device_id_type=LOGICAL,
+        ).start()
+
+    def index_to_row():
+        for o in range(1, n_col):
+            start(row_send.at[o], row_recv.at[opposite(o)], o, n_chunk)
+        row_recv[0] = row_send[0]
+
+    def index_to_col():
+        peers = pl.ds(1, n_col - 1)
+        pltpu.make_async_copy(row_send.at[peers], row_recv.at[peers], recv_sem.at[n_chunk]).wait()
+        for r in range(1, n_row):
+            back = opposite(r * n_col) // n_col
+            start(row_recv.at[:, r], col_recv.at[back], r * n_col, n_chunk + 1)
+        col_recv[0] = row_recv[:, 0]
+        pltpu.make_async_copy(row_send.at[peers], row_recv.at[peers], send_sem.at[n_chunk]).wait()
+
+    def index_done():
+        peers = pl.ds(0, n_row - 1)
+        for sem in (recv_sem, send_sem):
+            pltpu.make_async_copy(row_recv.at[:, peers], row_recv.at[:, peers], sem.at[n_chunk + 1]).wait()
+
     def inv(b, part):
         return (vh[b, part], vl[b, part])
 
@@ -317,7 +364,12 @@
             return [tuple(y[:TILE] for y in x), tuple(y[TILE:] for y in x)]
         return [tuple(y[:, :TILE] for y in x), tuple(y[:, TILE:] for y in x)]
 
-    n_chunk = len(sends)
+    with jax.named_scope("barwait"):
+        all_entered()
+        index_to_row()
+    with jax.named_scope("split"):
+        for p in range(len(pairs)):
+            oh[p], ol[p] = split(off[p])
     for ch in range(n_chunk):
         with jax.named_scope("fwd"):
             cols = slice(ch * CHUNK, (ch + 1) * CHUNK)
@@ -333,6 +385,9 @@
                     if j == b:
                         o = halves((oh[p], ol[p]), 1)
                         rhs[i] = (rhs[i] - mm3(o[0], fs[0])) - mm3(o[1], fs[1])
+        if ch == 0:
+            with jax.named_scope("idx"):
+                index_to_col()
         with jax.named_scope("bwd"):
             partial = []
             for b in reversed(range(n_big)):
@@ -360,10 +415,8 @@
                 some = slice(g * step, (g + 1) * step)
                 packed = mm(place[g * step * SLOTS : (g + 1) * step * SLOTS], update).reshape(step, SLOTS, CHUNK)
                 packed = jnp.concatenate([packed[:, :, :128], packed[:, :, 128:]], axis=1).astype(BF16)
-                sends[ch][some, : 2 * SLOTS] = packed
+                sends[ch][some] = packed
         with jax.named_scope("send"):
-            if ch == 0:
-                pl.semaphore_wait(barrier, n_holders - 1)
             dispatch(ch)
 
     stores = []
@@ -372,10 +425,11 @@
             arrived(ch)
         with jax.named_scope("final"):
             if ch == 0:
+                index_done()
                 pick0 = jnp.where(iota((8, 128), 1) == 0, 1.0, 0.0).astype(BF16)
-                named = mm_nt(pick0, recv0[:, 2 * SLOTS :].astype(F32).reshape(slots, 128).astype(BF16))[:1]
+                named = mm_nt(pick0, col_recv[...].astype(F32).reshape(slots, 128).astype(BF16))[:1]
                 gather = jnp.where(iota((owned, slots), 0).astype(F32) == named, 1.0, 0.0).astype(BF16)
-            got = recvs[ch][:, : 2 * SLOTS].astype(F32)
+            got = recvs[ch][...].astype(F32)
             got = jnp.concatenate(
                 [got[:, :SLOTS].reshape(slots, 128), got[:, SLOTS:].reshape(slots, 128)], axis=1
             )
@@ -393,6 +447,7 @@
     panel, factor, rows = coupling_panel[0], interior_factor[0], border_rows[0]
     n, width = panel.shape
     holders = lax.axis_size("row") * lax.axis_size("col")
+    n_col = lax.axis_size("col")
     n_tile, n_big, n_chunk = n // TILE, n // BIG, width // CHUNK
     pairs = n_big * (n_big - 1) // 2
     hbm = pl.BlockSpec(memory_space=pl.ANY)
@@ -413,15 +468,18 @@
             pltpu.VMEM((pairs, BIG, BIG), BF16),
             pltpu.VMEM((CHUNK, n), F32),
             pltpu.VMEM((holders * SLOTS, target_rows.shape[1]), BF16),
-            pltpu.VMEM((holders, 3 * SLOTS, 128), BF16),
-            pltpu.VMEM((holders, 3 * SLOTS, 128), BF16),
             pltpu.VMEM((holders, 2 * SLOTS, 128), BF16),
             pltpu.VMEM((holders, 2 * SLOTS, 128), BF16),
+            pltpu.VMEM((holders, 2 * SLOTS, 128), BF16),
+            pltpu.VMEM((holders, 2 * SLOTS, 128), BF16),
+            pltpu.VMEM((n_col, holders // n_col, SLOTS, 128), BF16),
+            pltpu.VMEM((n_col, holders // n_col, SLOTS, 128), BF16),
+            pltpu.VMEM((holders // n_col, n_col, SLOTS, 128), BF16),
             pltpu.VMEM(target_rows.shape, I32),
             pltpu.VMEM(border_block.shape, F32),
             pltpu.SemaphoreType.DMA((3 * n_tile + n_big + pairs + 3,)),
-            pltpu.SemaphoreType.DMA((n_chunk,)),
-            pltpu.SemaphoreType.DMA((n_chunk,)),
+            pltpu.SemaphoreType.DMA((n_chunk + 2,)),
+            pltpu.SemaphoreType.DMA((n_chunk + 2,)),
         ],
         compiler_params=pltpu.CompilerParams(
             collective_id=0, has_side_effects=True, vmem_limit_bytes=53 * 1024 * 1024

time: 36.1 us -> 41 us (1.14)
  Pallas kernels: 34.1 us -> 39.4 us
    pallas_call x1, Pallas kernels: 34.1 us -> 39.4 us  [local(): pl.pallas_call(kernel, out_shape=jax.ShapeDtypeStruct(border_block.shape,...]
where the time goes in v7:
time: 41 us; the launch traced here: 40.9 us
  Pallas kernels  39.4 us (96%)
  other arithmetic  0.87 us (2%)
  local copies, waits for them, and re-layouts  0.68 us (2%)
    pallas_call x1, Pallas kernels, local(): pl.pallas_call(kernel, out_shape=jax.ShapeDtypeStruct(border_block.shape,...  39.4 us
    sub x1, other arithmetic, local(): return border_block - assembled  0.87 us

profile of v7, /device:TPU:1, one launch (start us, length us, event | category | flops | bytes accessed | tf_op | source)
XLA Modules:
  0.0 40.9 jit_solution(12635813527172393838)
XLA Ops:
  0.0 0.0 copy-start
  0.0 0.7 %copy-done = s32[1,512]{1,0:T(1,128)S(1)} copy-done((s32[1,512]{1,0:T(1,128)S(1)}, s32[1,512]{1,0:T(1,128)}, u32[]{:S(2)}) %copy-start) | copy-done | bytes 2072
  0.7 0.0 copy-start.1
  0.7 39.4 %schur_panel.1 = f32[256,512]{1,0:T(8,128)S(1)} custom-call(bf16[1536,512]{1,0:T(8,128)(2,1)} %bitcast.4, f32[1536,1536]{1,0:T(8,128)} %bitcast.3, bf16[512,1536]{1,0:T(8,128)(2,1)} %bitcast.5, s32[1,512]{1,0:T(1,128)S(1)} %copy-done), custom_call_target="tpu_custom_call" | custom-call | tf_op jit(solution)/shard_map/schur_panel/pallas_call | solution.py:454
  40.0 0.0 copy-done.1
  40.1 0.9 %sub.3 = f32[256,512]{1,0:T(8,128)} subtract(f32[256,512]{1,0:T(8,128)S(1)} %copy-done.1, f32[256,512]{1,0:T(8,128)S(1)} %schur_panel.1) | non-fusion elementwise | flops 131072 | bytes 1572864 | tf_op jit(solution)/shard_map/sub | solution.py:489
Async XLA Ops:
  0.0 0.7 %copy-start = (s32[1,512]{1,0:T(1,128)S(1)}, s32[1,512]{1,0:T(1,128)}, u32[]{:S(2)}) copy-start(s32[1,512]{1,0:T(1,128)} %target_hbm.1) | copy-start | bytes 6148
  0.7 39.4 %copy-start.1 = (f32[256,512]{1,0:T(8,128)S(1)}, f32[256,512]{1,0:T(8,128)}, u32[]{:S(2)}) copy-start(f32[256,512]{1,0:T(8,128)} %param.9) | copy-start | bytes 1572868

commit v8 on v6

--- a/solution.py
+++ b/solution.py
@@ -105,10 +105,11 @@
     return [base[:, t : t + 128] for t in range(0, base.shape[1], 128)]
 
 
-def invert_small(diag, tiles):
+def invert_small(diag, tiles, between):
     small = small_tiles(diag)
     size = BASE
     while size < 128:
+        between()
         group = iota((size, 128), 1) // size
         even = group % 2 == 0
         corners = []
@@ -242,14 +243,26 @@
     load(panel_hbm, panel)
     load(rows_hbm, rows)
 
-    with jax.named_scope("greet"):
-        barrier = pltpu.get_barrier_semaphore()
-        for o in offsets:
-            pl.semaphore_signal(barrier, inc=1, device_id=device_at(o), device_id_type=LOGICAL)
+    barrier = pltpu.get_barrier_semaphore()
+
+    @pl.when(me != 0)
+    def _():
+        pl.semaphore_signal(barrier, inc=1, device_id=0, device_id_type=LOGICAL)
+
+    def collect():
+        @pl.when(me == 0)
+        def _():
+            pl.semaphore_wait(barrier, n_holders - 1)
+            for o in range(n_holders - 1, 0, -1):
+                pl.semaphore_signal(barrier, inc=1, device_id=o, device_id_type=LOGICAL)
+
+    def all_entered():
+        @pl.when(me != 0)
+        def _():
+            pl.semaphore_wait(barrier, 1)
 
     first, second = 2 * n_tile + 1, 3 * n_tile + n_big + 1
-    for cp in loads[:first]:
-        cp.wait()
+    loads[0].wait()
     with jax.named_scope("place"):
         sent = target_ref.shape[1]
         target = jnp.broadcast_to(target_ref[...], (8, sent))
@@ -271,9 +284,16 @@
         found = mm_nt(placed, described)
         index = found[:, :128] + EMPTY * (1.0 - found[:, 128:])
         send0[:, 2 * SLOTS :] = index.reshape(n_holders, SLOTS, 128).astype(BF16)
+    for cp in loads[1:first]:
+        cp.wait()
+    waiting = loads[first:second]
+
+    def between():
+        waiting.pop(0).wait()
+
     with jax.named_scope("small"):
-        small = invert_small(diag, invert_bases(diag))
-    for cp in loads[first:second]:
+        small = invert_small(diag, invert_bases(diag), between)
+    for cp in waiting:
         cp.wait()
     with jax.named_scope("merge"):
         inverse = invert_tiles(diag, small)
@@ -286,6 +306,8 @@
                 ref[b, 2] = bottom[i]
     for cp in loads[second:]:
         cp.wait()
+    with jax.named_scope("collect"):
+        collect()
     with jax.named_scope("split"):
         for p in range(len(pairs)):
             oh[p], ol[p] = split(off[p])
@@ -363,7 +385,7 @@
                 sends[ch][some, : 2 * SLOTS] = packed
         with jax.named_scope("send"):
             if ch == 0:
-                pl.semaphore_wait(barrier, n_holders - 1)
+                all_entered()
             dispatch(ch)
 
     stores = []

time: 36.1 us -> 36.9 us (1.022)
  Pallas kernels: 34.1 us -> 34.8 us
    pallas_call x1, Pallas kernels: 34.1 us -> 34.8 us  [local(): pl.pallas_call(kernel, out_shape=jax.ShapeDtypeStruct(border_block.shape,...]
where the time goes in v8:
time: 36.9 us; the launch traced here: 36.4 us
  Pallas kernels  34.8 us (94%)
  other arithmetic  0.87 us (2%)
  local copies, waits for them, and re-layouts  0.68 us (2%)
    pallas_call x1, Pallas kernels, local(): pl.pallas_call(kernel, out_shape=jax.ShapeDtypeStruct(border_block.shape,...  34.8 us
    sub x1, other arithmetic, local(): return border_block - assembled  0.87 us

profile of v8, /device:TPU:1, one launch (start us, length us, event | category | flops | bytes accessed | tf_op | source)
XLA Modules:
  0.0 36.4 jit_solution(1439181647937277075)
XLA Ops:
  0.0 0.0 copy-start
  0.0 0.7 %copy-done = s32[1,512]{1,0:T(1,128)S(1)} copy-done((s32[1,512]{1,0:T(1,128)S(1)}, s32[1,512]{1,0:T(1,128)}, u32[]{:S(2)}) %copy-start) | copy-done | bytes 2072
  0.7 0.0 copy-start.1
  0.7 34.8 %schur_panel.1 = f32[256,512]{1,0:T(8,128)S(1)} custom-call(bf16[1536,512]{1,0:T(8,128)(2,1)} %bitcast.4, f32[1536,1536]{1,0:T(8,128)} %bitcast.3, bf16[512,1536]{1,0:T(8,128)(2,1)} %bitcast.5, s32[1,512]{1,0:T(1,128)S(1)} %copy-done), custom_call_target="tpu_custom_call" | custom-call | tf_op jit(solution)/shard_map/schur_panel/pallas_call | solution.py:421
  35.5 0.0 copy-done.1
  35.5 0.9 %sub.3 = f32[256,512]{1,0:T(8,128)} subtract(f32[256,512]{1,0:T(8,128)S(1)} %copy-done.1, f32[256,512]{1,0:T(8,128)S(1)} %schur_panel.1) | non-fusion elementwise | flops 131072 | bytes 1572864 | tf_op jit(solution)/shard_map/sub | solution.py:453
Async XLA Ops:
  0.0 0.7 %copy-start = (s32[1,512]{1,0:T(1,128)S(1)}, s32[1,512]{1,0:T(1,128)}, u32[]{:S(2)}) copy-start(s32[1,512]{1,0:T(1,128)} %target_hbm.1) | copy-start | bytes 6148
  0.7 34.8 %copy-start.1 = (f32[256,512]{1,0:T(8,128)S(1)}, f32[256,512]{1,0:T(8,128)}, u32[]{:S(2)}) copy-start(f32[256,512]{1,0:T(8,128)} %param.9) | copy-start | bytes 1572868

commit v9 on v6

--- a/solution.py
+++ b/solution.py
@@ -200,16 +200,20 @@
 
 def kernel(
     panel_hbm, factor_hbm, rows_hbm, target_hbm, out_ref,
-    panel, rows, diag, sub, off, vh, vl, oh, ol, fwd, place, send0, recv0, send1, recv1, target_ref, result,
+    panel, rows, diag, sub, off, vh, vl, oh, ol, fwd, place, send0, recv0, send1, recv1,
+    row_send, row_recv, col_send, col_recv, target_ref, result,
     load_sem, send_sem, recv_sem,
 ):
     n_holders = lax.axis_size("row") * lax.axis_size("col")
     me = lax.axis_index("row") * lax.axis_size("col") + lax.axis_index("col")
     here = parts_of(me)
+    n_col = SIDE * SIDE
+    n_row = n_holders // n_col
     n_big = off.shape[0]
     n_tile = diag.shape[0]
     owned = result.shape[0]
     sends, recvs = (send0, send1), (recv0, recv1)
+    n_chunk = len(sends)
     pairs = [(1, 0), (2, 0), (2, 1)]
     offsets = send_order(n_holders)
     ahead = [[lax.rem(c + d, n) for d in range(n)] for c, n in zip(here, SIZES)]
@@ -270,7 +274,11 @@
         ).astype(BF16)
         found = mm_nt(placed, described)
         index = found[:, :128] + EMPTY * (1.0 - found[:, 128:])
-        send0[:, 2 * SLOTS :] = index.reshape(n_holders, SLOTS, 128).astype(BF16)
+        index = jnp.where(iota((slots, 128), 1) == iota((slots, 128), 0) % SLOTS, index, 0.0).astype(BF16)
+        turn = iota((n_holders, slots), 0)
+        turn = turn % n_row * n_col + turn // n_row
+        collect = jnp.where(turn == iota((n_holders, slots), 1) // SLOTS, 1.0, 0.0).astype(BF16)
+        row_send[...] = mm(collect, index).reshape(n_col, n_row, 128)
     with jax.named_scope("small"):
         small = invert_small(diag, invert_bases(diag))
     for cp in loads[first:second]:
@@ -309,6 +317,34 @@
     def left_device(ch):
         pltpu.make_async_copy(sends[ch].at[others], recvs[ch].at[others], send_sem.at[ch]).wait()
 
+    def start(src, dst, o, at):
+        pltpu.make_async_remote_copy(
+            src_ref=src, dst_ref=dst, send_sem=send_sem.at[at], recv_sem=recv_sem.at[at],
+            device_id=device_at(o), device_id_type=LOGICAL,
+        ).start()
+
+    col_peers, row_peers = pl.ds(1, n_col - 1), pl.ds(1, n_row - 1)
+
+    def index_to_row():
+        for o in range(1, n_col):
+            start(row_send.at[o], row_recv.at[opposite(o)], o, n_chunk)
+        row_recv[0] = row_send[0]
+
+    def index_to_col():
+        pltpu.make_async_copy(row_send.at[col_peers], row_recv.at[col_peers], recv_sem.at[n_chunk]).wait()
+        turn = iota((n_holders, n_holders), 0)
+        turn = turn % n_col * n_row + turn // n_col
+        turned = jnp.where(turn == iota((n_holders, n_holders), 1), 1.0, 0.0).astype(BF16)
+        col_send[...] = mm(turned, row_recv[...].reshape(n_holders, 128).astype(BF16)).reshape(n_row, n_col, 128)
+        for r in range(1, n_row):
+            start(col_send.at[r], col_recv.at[opposite(r * n_col) // n_col], r * n_col, n_chunk + 1)
+        col_recv[0] = col_send[0]
+
+    def index_done():
+        pltpu.make_async_copy(row_send.at[col_peers], row_recv.at[col_peers], send_sem.at[n_chunk]).wait()
+        for sem in (recv_sem, send_sem):
+            pltpu.make_async_copy(col_send.at[row_peers], col_recv.at[row_peers], sem.at[n_chunk + 1]).wait()
+
     def inv(b, part):
         return (vh[b, part], vl[b, part])
 
@@ -333,6 +369,12 @@
                     if j == b:
                         o = halves((oh[p], ol[p]), 1)
                         rhs[i] = (rhs[i] - mm3(o[0], fs[0])) - mm3(o[1], fs[1])
+        with jax.named_scope("idx"):
+            if ch == 0:
+                pl.semaphore_wait(barrier, n_holders - 1)
+                index_to_row()
+            else:
+                index_to_col()
         with jax.named_scope("bwd"):
             partial = []
             for b in reversed(range(n_big)):
@@ -360,10 +402,8 @@
                 some = slice(g * step, (g + 1) * step)
                 packed = mm(place[g * step * SLOTS : (g + 1) * step * SLOTS], update).reshape(step, SLOTS, CHUNK)
                 packed = jnp.concatenate([packed[:, :, :128], packed[:, :, 128:]], axis=1).astype(BF16)
-                sends[ch][some, : 2 * SLOTS] = packed
+                sends[ch][some] = packed
         with jax.named_scope("send"):
-            if ch == 0:
-                pl.semaphore_wait(barrier, n_holders - 1)
             dispatch(ch)
 
     stores = []
@@ -372,10 +412,13 @@
             arrived(ch)
         with jax.named_scope("final"):
             if ch == 0:
-                pick0 = jnp.where(iota((8, 128), 1) == 0, 1.0, 0.0).astype(BF16)
-                named = mm_nt(pick0, recv0[:, 2 * SLOTS :].astype(F32).reshape(slots, 128).astype(BF16))[:1]
+                index_done()
+                names = col_recv[...].reshape(n_holders, 128).astype(BF16)
+                lanes = jnp.where(iota((128, slots), 0) == iota((128, slots), 1) % SLOTS, 1.0, 0.0).astype(BF16)
+                mine = iota((n_holders, slots), 0) == iota((n_holders, slots), 1) // SLOTS
+                named = jnp.sum(jnp.where(mine, mm(names, lanes), 0.0), axis=0, keepdims=True)
                 gather = jnp.where(iota((owned, slots), 0).astype(F32) == named, 1.0, 0.0).astype(BF16)
-            got = recvs[ch][:, : 2 * SLOTS].astype(F32)
+            got = recvs[ch][...].astype(F32)
             got = jnp.concatenate(
                 [got[:, :SLOTS].reshape(slots, 128), got[:, SLOTS:].reshape(slots, 128)], axis=1
             )
@@ -393,6 +436,7 @@
     panel, factor, rows = coupling_panel[0], interior_factor[0], border_rows[0]
     n, width = panel.shape
     holders = lax.axis_size("row") * lax.axis_size("col")
+    n_col = lax.axis_size("col")
     n_tile, n_big, n_chunk = n // TILE, n // BIG, width // CHUNK
     pairs = n_big * (n_big - 1) // 2
     hbm = pl.BlockSpec(memory_space=pl.ANY)
@@ -413,15 +457,19 @@
             pltpu.VMEM((pairs, BIG, BIG), BF16),
             pltpu.VMEM((CHUNK, n), F32),
             pltpu.VMEM((holders * SLOTS, target_rows.shape[1]), BF16),
-            pltpu.VMEM((holders, 3 * SLOTS, 128), BF16),
-            pltpu.VMEM((holders, 3 * SLOTS, 128), BF16),
             pltpu.VMEM((holders, 2 * SLOTS, 128), BF16),
             pltpu.VMEM((holders, 2 * SLOTS, 128), BF16),
+            pltpu.VMEM((holders, 2 * SLOTS, 128), BF16),
+            pltpu.VMEM((holders, 2 * SLOTS, 128), BF16),
+            pltpu.VMEM((n_col, holders // n_col, 128), F32),
+            pltpu.VMEM((n_col, holders // n_col, 128), F32),
+            pltpu.VMEM((holders // n_col, n_col, 128), F32),
+            pltpu.VMEM((holders // n_col, n_col, 128), F32),
             pltpu.VMEM(target_rows.shape, I32),
             pltpu.VMEM(border_block.shape, F32),
             pltpu.SemaphoreType.DMA((3 * n_tile + n_big + pairs + 3,)),
-            pltpu.SemaphoreType.DMA((n_chunk,)),
-            pltpu.SemaphoreType.DMA((n_chunk,)),
+            pltpu.SemaphoreType.DMA((n_chunk + 2,)),
+            pltpu.SemaphoreType.DMA((n_chunk + 2,)),
         ],
         compiler_params=pltpu.CompilerParams(
             collective_id=0, has_side_effects=True, vmem_limit_bytes=53 * 1024 * 1024

time: 36.1 us -> 35.5 us (0.983)
  Pallas kernels: 34.1 us -> 33.4 us
    pallas_call x1, Pallas kernels: 34.1 us -> 33.4 us  [local(): pl.pallas_call(kernel, out_shape=jax.ShapeDtypeStruct(border_block.shape,...]
where the time goes in v9:
time: 35.5 us; the launch traced here: 35 us
  Pallas kernels  33.4 us (94%)
  other arithmetic  0.87 us (2%)
  local copies, waits for them, and re-layouts  0.68 us (2%)
    pallas_call x1, Pallas kernels, local(): pl.pallas_call(kernel, out_shape=jax.ShapeDtypeStruct(border_block.shape,...  33.4 us
    sub x1, other arithmetic, local(): return border_block - assembled  0.87 us

profile of v9, /device:TPU:1, one launch (start us, length us, event | category | flops | bytes accessed | tf_op | source)
XLA Modules:
  0.0 35.0 jit_solution(5645767063252589034)
XLA Ops:
  0.0 0.0 copy-start
  0.0 0.7 %copy-done = s32[1,512]{1,0:T(1,128)S(1)} copy-done((s32[1,512]{1,0:T(1,128)S(1)}, s32[1,512]{1,0:T(1,128)}, u32[]{:S(2)}) %copy-start) | copy-done | bytes 2072
  0.7 0.0 copy-start.1
  0.7 33.4 %schur_panel.1 = f32[256,512]{1,0:T(8,128)S(1)} custom-call(bf16[1536,512]{1,0:T(8,128)(2,1)} %bitcast.4, f32[1536,1536]{1,0:T(8,128)} %bitcast.3, bf16[512,1536]{1,0:T(8,128)(2,1)} %bitcast.5, s32[1,512]{1,0:T(1,128)S(1)} %copy-done), custom_call_target="tpu_custom_call" | custom-call | tf_op jit(solution)/shard_map/schur_panel/pallas_call | solution.py:443
  34.1 0.0 copy-done.1
  34.1 0.9 %sub.3 = f32[256,512]{1,0:T(8,128)} subtract(f32[256,512]{1,0:T(8,128)S(1)} %copy-done.1, f32[256,512]{1,0:T(8,128)S(1)} %schur_panel.1) | non-fusion elementwise | flops 131072 | bytes 1572864 | tf_op jit(solution)/shard_map/sub | solution.py:479
Async XLA Ops:
  0.0 0.7 %copy-start = (s32[1,512]{1,0:T(1,128)S(1)}, s32[1,512]{1,0:T(1,128)}, u32[]{:S(2)}) copy-start(s32[1,512]{1,0:T(1,128)} %target_hbm.1) | copy-start | bytes 6148
  0.7 33.4 %copy-start.1 = (f32[256,512]{1,0:T(8,128)S(1)}, f32[256,512]{1,0:T(8,128)}, u32[]{:S(2)}) copy-start(f32[256,512]{1,0:T(8,128)} %param.9) | copy-start | bytes 1572868
